TPU v7x, 64 devices: a 2x2x8 block of a 4x4x8 slice. The times are simulated.
64 devices in a mesh: dp: 4 (over x, y), ep: 16 (over z, core).
Axes of the slice: x: 2, y: 2, z: 8, core: 2. Of those that a mesh axis runs over, the one named last changes fastest.
The devices are a block of a 4x4x8 slice.
Arguments:
- x_tok: bfloat16 [4096, 2560], P(('dp', 'ep')), parts along dimension 0
- topk_idx: int32 [4096, 6], P(('dp', 'ep')), parts along dimension 0
- topk_w: float32 [4096, 6], P(('dp', 'ep')), parts along dimension 0
- w_in: bfloat16 [64, 2560, 1536], P('ep')
- w_out: bfloat16 [64, 1536, 2560], P('ep')
- shared_in: bfloat16 [2560, 3072], replicated
- shared_out: bfloat16 [3072, 2560], replicated
Outputs:
- output: bfloat16 [4096, 2560], P(('dp', 'ep')), parts along dimension 0
There are 4 independent parts. A program takes and returns all parts, laid end to end along the dimension named above; an argument that names none is the same for every part.
All inputs are finite; a program needn't handle non-finite values.
Results may differ from a plain program's by a relative error of at most 0.001.
Values are sent between devices in bfloat16 or wider.
A program may use at most 768 MiB of HBM per device.

v0:
```python
import jax
import jax.numpy as jnp
from jax import lax
from jax.sharding import PartitionSpec as P

LOAD_MULT = 3


def slot_tables(topk_idx, topk_w, num_experts, slot_cap):
    tok_rows, top_k = topk_idx.shape
    expert_hot = (topk_idx[:, :, None] == jnp.arange(num_experts, dtype=jnp.int32)).astype(jnp.int32)
    running = jnp.cumsum(expert_hot.reshape(tok_rows * top_k, num_experts), axis=0)
    slot_pos = jnp.sum(running.reshape(tok_rows, top_k, num_experts) * expert_hot, axis=2) - 1
    slot_hot = (slot_pos[:, :, None] == jnp.arange(slot_cap, dtype=jnp.int32)).astype(jnp.bfloat16)
    gate_hot = expert_hot.astype(jnp.bfloat16) * topk_w.astype(jnp.bfloat16)[:, :, None]
    combine = jnp.einsum('tje,tjc->tec', gate_hot, slot_hot, preferred_element_type=jnp.float32).astype(jnp.bfloat16)
    dispatch = (combine != 0).astype(jnp.bfloat16)
    return combine, dispatch


def solution(mesh):
    group_size = mesh.shape['ep']

    def local_layer(x_loc, idx_loc, gate_loc, w_in, w_out, shared_in, shared_out):
        tok_rows, top_k = idx_loc.shape
        num_experts = w_in.shape[0] * group_size
        slot_cap = min(tok_rows, LOAD_MULT * tok_rows * top_k // num_experts)
        combine, dispatch = slot_tables(idx_loc, gate_loc, num_experts, slot_cap)
        send_rows = jnp.einsum('tec,tm->ecm', dispatch, x_loc, preferred_element_type=jnp.float32).astype(jnp.bfloat16)
        recv_rows = lax.all_to_all(send_rows, 'ep', 0, 1, tiled=True)
        hidden = jax.nn.gelu(jnp.einsum('erm,emf->erf', recv_rows, w_in, preferred_element_type=jnp.float32), approximate=True).astype(jnp.bfloat16)
        expert_out = jnp.einsum('erf,efm->erm', hidden, w_out, preferred_element_type=jnp.float32).astype(jnp.bfloat16)
        back_rows = lax.all_to_all(expert_out, 'ep', 1, 0, tiled=True)
        routed = jnp.einsum('tec,ecm->tm', combine, back_rows, preferred_element_type=jnp.float32)
        shared_hidden = jax.nn.gelu(jnp.dot(x_loc, shared_in, preferred_element_type=jnp.float32), approximate=True).astype(jnp.bfloat16)
        shared_val = jnp.dot(shared_hidden, shared_out, preferred_element_type=jnp.float32)
        return (routed + shared_val).astype(jnp.bfloat16)

    tok_spec = P(('dp', 'ep'), None)
    expert_spec = P('ep', None, None)
    whole_spec = P(None, None)
    return jax.shard_map(local_layer, mesh=mesh, in_specs=(tok_spec, tok_spec, tok_spec, expert_spec, expert_spec, whole_spec, whole_spec), out_specs=tok_spec, check_vma=False)
```

profile of v0, /device:TPU:21, one launch (start us, length us, event | category | flops | bytes accessed | tf_op | source)
XLA Modules:
  0.0 418.5 jit_solution(3600209984251454264)
XLA Ops:
  0.0 0.0 copy-start
  0.0 0.8 copy.37
  0.8 0.1 eq.53
  1.0 0.1 eq.49
  1.1 0.7 convert_element_type.36
  1.8 0.1 copy.38
  1.9 0.9 reduce-window.6
  2.8 0.2 slice_reduce_fusion
  3.1 0.1 fusion.35
  3.2 0.1 sub.7
  3.4 0.8 fusion.28
  4.2 0.0 copy-done
  4.2 4.3 %convolution_convert_fusion.1 = bf16[64,18,2560]{2,0,1:T(8,128)(2,1)} fusion(bf16[64,2560]{1,0:T(8,128)(2,1)S(1)} %copy-done, bf16[64,64,18]{1,2,0:T(8,128)(2,1)S(1)} %fusion.28), kind=kOutput, calls=%fused_computation.10 | convolution fusion | flops 380510208 | bytes 6373376 | tf_op jit(solution)/shard_map/tec,tm->ecm/dot_general | solution.py:29
  8.4 6.0 %copy.44 = bf16[64,18,2560]{2,1,0:T(8,128)(2,1)S(1)} copy(bf16[64,18,2560]{2,0,1:T(8,128)(2,1)} %convolution_convert_fusion.1) | data formatting | bytes 11796480 | tf_op jit(solution)/shard_map/convert_element_type | solution.py:29
  14.4 184.4 %all_to_all.36 = bf16[64,18,2560]{2,1,0:T(8,128)(2,1)} all-to-all(bf16[64,18,2560]{2,1,0:T(8,128)(2,1)S(1)} %copy.44), channel_id=1, replica_groups=mesh['dp'=4,'ep'=16] {'ep'}, dimensions={0} | all-to-all | bytes 11796480 | tf_op jit(solution)/shard_map/all_to_all | solution.py:30
  198.8 8.8 %copy.45 = bf16[16,4,18,2560]{3,1,2,0:T(4,128)(2,1)} copy(bf16[16,4,18,2560]{3,2,1,0:T(8,128)(2,1)} %bitcast.41) | data formatting | bytes 11796480 | tf_op jit(solution)/shard_map/all_to_all | solution.py:30
  207.6 30.2 %convolution_convert_fusion = bf16[4,288,2560]{2,1,0:T(8,128)(2,1)} fusion(bf16[4,1536,2560]{2,1,0:T(8,128)(2,1)} %param.11, bf16[4,2560,1536]{2,1,0:T(8,128)(2,1)} %param.10, bf16[4,288,2560]{2,0,1:T(4,128)(2,1)} %bitcast.43), kind=kOutput, calls=%fused_computation.9 | convolution fusion | flops 18138267648 | bytes 74711040 | tf_op jit(solution)/shard_map/erf,efm->erm/dot_general | solution.py:32
  237.8 7.2 %copy.47 = bf16[4,288,2560]{2,0,1:T(4,128)(2,1)S(1)} copy(bf16[4,288,2560]{2,1,0:T(8,128)(2,1)} %convolution_convert_fusion) | data formatting | bytes 11796480 | tf_op jit(solution)/shard_map/convert_element_type | solution.py:32
  245.1 134.9 %all_to_all.37 = bf16[4,288,2560]{2,0,1:T(4,128)(2,1)} all-to-all(bf16[4,288,2560]{2,0,1:T(4,128)(2,1)S(1)} %copy.47), channel_id=1, replica_groups=mesh['dp'=4,'ep'=16] {'ep'}, dimensions={1} | all-to-all | bytes 11796480 | tf_op jit(solution)/shard_map/all_to_all | solution.py:33
  380.0 8.1 %copy.48 = bf16[16,4,18,2560]{3,1,0,2:T(4,128)(2,1)} copy(bf16[16,4,18,2560]{3,1,2,0:T(4,128)(2,1)} %bitcast.42) | data formatting | bytes 11796480 | tf_op jit(solution)/shard_map/all_to_all | solution.py:33
  388.0 10.2 %all_to_all.33 = bf16[64,18,2560]{2,0,1:T(8,128)(2,1)} reshape(bf16[16,4,18,2560]{3,1,0,2:T(4,128)(2,1)} %copy.48) | data formatting | bytes 11796480 | tf_op jit(solution)/shard_map/all_to_all | solution.py:33
  398.3 3.8 convolution_bitcast_fusion
  402.1 16.4 %fusion.12 = bf16[64,2560]{1,0:T(8,128)(2,1)} fusion(f32[64,2560]{1,0:T(8,128)S(1)} %convolution_bitcast_fusion, bf16[3072,2560]{1,0:T(8,128)(2,1)} %param.13, bf16[64,2560]{1,0:T(8,128)(2,1)S(1)} %copy-done, bf16[2560,3072]{1,0:T(8,128)(2,1)} %param.12), kind=kOutput, calls=%fused_computation.15 | convolution fusion | flops 2015363072 | bytes 32768000 | tf_op jit(solution)/shard_map/dot_general | solution.py:36
  (3 shorter events, 0.1 us)
Async XLA Ops:
  0.0 4.2 copy-start
where the time goes:
time: 419 us; the launch traced here: 418 us
  blocking collectives  319 us (76%)
  matrix products  55.5 us (13%)
  local copies, waits for them, and re-layouts  41.9 us (10%)
    all_to_all x1, blocking collectives, local_layer(): recv_rows = lax.all_to_all(send_rows, 'ep', 0, 1, tiled=True)  184 us
    all_to_all x1, blocking collectives, local_layer(): back_rows = lax.all_to_all(expert_out, 'ep', 1, 0, tiled=True)  135 us
    dot_general x1, matrix products, local_layer(): jnp.einsum('erf,efm->erm', hidden, w_out, preferred_element_type=jnp.floa...  30.2 us
    all_to_all x2, local copies, waits for them, and re-layouts, local_layer(): back_rows = lax.all_to_all(expert_out, 'ep', 1, 0, tiled=True)  18.3 us
    dot_general x1, matrix products, local_layer(): jnp.dot(shared_hidden, shared_out, preferred_element_type=jnp.float32)  16.4 us
    all_to_all x1, local copies, waits for them, and re-layouts, local_layer(): recv_rows = lax.all_to_all(send_rows, 'ep', 0, 1, tiled=True)  8.84 us

commit v1 on v0

v1 whole, which is shorter than its diff:
```python
import jax
import jax.numpy as jnp
from jax import lax
from jax.sharding import PartitionSpec as P

LOAD_MULT = 3


def solution(mesh):
    group_size = mesh.shape['ep']

    def local_layer(x_loc, idx_loc, gate_loc, w_in, w_out, shared_in, shared_out):
        tok_rows, top_k = idx_loc.shape
        own_experts = w_in.shape[0]
        num_experts = own_experts * group_size
        slot_cap = min(tok_rows, LOAD_MULT * tok_rows * top_k // num_experts)
        x_all = lax.all_gather(x_loc, 'ep', axis=0, tiled=True)
        picks = (idx_loc[:, :, None] == jnp.arange(num_experts, dtype=jnp.int32))
        picked = jnp.any(picks, axis=1)
        rank = jnp.cumsum(picked.astype(jnp.int32), axis=0) - 1
        gates = jnp.sum(jnp.where(picks, gate_loc.astype(jnp.bfloat16).astype(jnp.float32)[:, :, None], 0.0), axis=1)
        code = jnp.where(picked, rank, -1).astype(jnp.float32)
        table = jnp.stack([code, gates], axis=0).reshape(2, tok_rows, group_size, own_experts)
        table = lax.all_to_all(table, 'ep', 2, 1, tiled=True)
        table = table.reshape(2, group_size, tok_rows, own_experts)
        code_all, gate_all = table[0], table[1]
        hot = (code_all[:, :, :, None] == jnp.arange(slot_cap, dtype=jnp.float32))
        own = jnp.eye(group_size, dtype=jnp.bool_)
        disp = (hot[:, :, :, None, :] & own[:, None, None, :, None])
        combine = jnp.where(disp, gate_all[:, :, :, None, None], 0.0).astype(jnp.bfloat16)
        rows = group_size * slot_cap
        disp = disp.astype(jnp.bfloat16).reshape(group_size * tok_rows, own_experts, rows)
        combine = combine.reshape(group_size * tok_rows, own_experts, rows)
        recv_rows = jnp.einsum('ter,tm->erm', disp, x_all, preferred_element_type=jnp.float32).astype(jnp.bfloat16)
        hidden = jax.nn.gelu(jnp.einsum('erm,emf->erf', recv_rows, w_in, preferred_element_type=jnp.float32), approximate=True).astype(jnp.bfloat16)
        expert_out = jnp.einsum('erf,efm->erm', hidden, w_out, preferred_element_type=jnp.float32).astype(jnp.bfloat16)
        partial = jnp.einsum('ter,erm->tm', combine, expert_out, preferred_element_type=jnp.float32)
        routed = lax.psum_scatter(partial, 'ep', scatter_dimension=0, tiled=True)
        shared_hidden = jax.nn.gelu(jnp.dot(x_loc, shared_in, preferred_element_type=jnp.float32), approximate=True).astype(jnp.bfloat16)
        shared_val = jnp.dot(shared_hidden, shared_out, preferred_element_type=jnp.float32)
        return (routed + shared_val).astype(jnp.bfloat16)

    tok_spec = P(('dp', 'ep'), None)
    expert_spec = P('ep', None, None)
    whole_spec = P(None, None)
    return jax.shard_map(local_layer, mesh=mesh, in_specs=(tok_spec, tok_spec, tok_spec, expert_spec, expert_spec, whole_spec, whole_spec), out_specs=tok_spec, check_vma=False)
```

time: 419 us -> 198 us (0.47)
  blocking collectives: 319 us -> 0 us
  waiting for transfers between devices: 0 us -> 83.2 us
  local copies, waits for them, and re-layouts: 41.9 us -> 11.1 us
  between operations: 0.05 us -> 13.6 us
  matrix products: 55.5 us -> 67.6 us
  starting transfers between devices: 0 us -> 10.8 us
  other arithmetic: 1.77 us -> 9.78 us
    all_to_all x2 -> x0, blocking collectives: 319 us -> none  [the longest x1 184 us: local_layer(): recv_rows = lax.all_to_all(send_rows, 'ep', 0, 1, tiled=True)]
    reduce_scatter x0 -> x1, waiting for transfers between devices: none -> 66.7 us  [local_layer(): routed = lax.psum_scatter(partial, 'ep', scatter_dimension=0, tiled=True)]
    all_to_all x3 -> x2, local copies, waits for them, and re-layouts: 27.1 us -> 0.6 us  [local_layer(): table = lax.all_to_all(table, 'ep', 2, 1, tiled=True)]
    dot_general x3 -> x2, matrix products: 8.89 us -> 22.2 us  [the longest x1 11.5 us: local_layer(): jnp.einsum('ter,erm->tm', combine, expert_out, preferred_element_type=jnp...]
    convert_element_type x3 -> x1, local copies, waits for them, and re-layouts: 13.3 us -> 0.33 us  [local_layer(): rank = jnp.cumsum(picked.astype(jnp.int32), axis=0) - 1]
    all_to_all x0 -> x1, starting transfers between devices: none -> 10.7 us  [local_layer(): table = lax.all_to_all(table, 'ep', 2, 1, tiled=True)]
    all_gather x0 -> x1, waiting for transfers between devices: none -> 10.3 us  [local_layer(): x_all = lax.all_gather(x_loc, 'ep', axis=0, tiled=True)]
    and x0 -> x4, local copies, waits for them, and re-layouts: none -> 7.95 us  [local_layer(): disp = hot[:, :, :, None, :] & own[:, None, None, :, None]]
  transfers between devices with their start and end apart: 0 -> 3, of which waited for: 0 -> 3; matrix products, arithmetic and copies ran while one was open for 0% -> 11% of each run, Pallas kernels for 0% -> 0%
where the time goes in v1:
time: 198 us; the launch traced here: 196 us
  waiting for transfers between devices  83.2 us (42%)
  matrix products  67.6 us (34%)
  between operations  13.6 us (7%)
  local copies, waits for them, and re-layouts  11.1 us (6%)
  starting transfers between devices  10.8 us (5%)
  other arithmetic  9.78 us (5%)
    reduce_scatter x1, waiting for transfers between devices, local_layer(): routed = lax.psum_scatter(partial, 'ep', scatter_dimension=0, tiled=True)  66.7 us
    dot_general x1, matrix products, local_layer(): jnp.einsum('erf,efm->erm', hidden, w_out, preferred_element_type=jnp.floa...  29 us
    dot_general x1, matrix products, local_layer(): jnp.dot(shared_hidden, shared_out, preferred_element_type=jnp.float32)  16.5 us
    dot_general x1, matrix products, local_layer(): jnp.einsum('ter,erm->tm', combine, expert_out, preferred_element_type=jnp...  11.5 us
    all_to_all x1, starting transfers between devices, local_layer(): table = lax.all_to_all(table, 'ep', 2, 1, tiled=True)  10.7 us
    dot_general x1, matrix products, local_layer(): jnp.einsum('ter,tm->erm', disp, x_all, preferred_element_type=jnp.float32)  10.7 us
    all_gather x1, waiting for transfers between devices, local_layer(): x_all = lax.all_gather(x_loc, 'ep', axis=0, tiled=True)  10.3 us
    and x4, local copies, waits for them, and re-layouts, local_layer(): disp = hot[:, :, :, None, :] & own[:, None, None, :, None]  7.95 us
  transfers between devices with their start and end apart: 3, of which 3 were waited for; matrix products, arithmetic and copies ran while one was open for 11% of the time, Pallas kernels for 0%

profile of v1, /device:TPU:21, one launch (start us, length us, event | category | flops | bytes accessed | tf_op | source)
XLA Modules:
  0.0 196.1 jit_solution(1230652049676698384)
XLA Ops:
  6.6 0.7 all-gather.2.cloned.1.call-update
  7.3 0.8 fusion.33
  8.2 0.4 copy.29
  8.6 0.7 convert_convert_fusion
  9.3 0.9 select_reduce_fusion
  10.2 0.3 copy.28
  10.6 0.3 copy.31
  10.9 6.5 %select_convert_fusion.2 = f32[1,64,16,4]{3,2,1,0:T(8,128)S(1)} fusion(pred[1,64,16,4]{3,2,1,0:T(8,128)(4,1)S(1)} %copy.29, s32[1,64,16,4]{3,2,1,0:T(8,128)S(1)} %copy.28), kind=kOutput, calls=%fused_computation.36 | output fusion | flops 270336 | bytes 36864 | tf_op jit(solution)/shard_map/jit(cumsum)/reduce_window_sum | solution.py:20
  17.5 0.5 copy.32
  18.0 0.7 reshape.64
  18.7 10.7 %all-to-all-start = ((f32[16,1,512]{2,1,0:T(1,128)}), f32[16,1,512]{2,1,0:T(1,128)S(1)}, u32[]{:S(2)}, u32[]{:S(2)}) async-start(f32[16,1,512]{2,1,0:T(1,128)} %reshape.64), calls=%async_computation | async-start | bytes 65536 | tf_op jit(solution)/shard_map/all_to_all | solution.py:24
  29.5 0.2 and.23
  29.7 1.6 and.24
  31.3 5.4 %all-to-all-done = f32[16,1,512]{2,1,0:T(1,128)S(1)} async-done(((f32[16,1,512]{2,1,0:T(1,128)}), f32[16,1,512]{2,1,0:T(1,128)S(1)}, u32[]{:S(2)}, u32[]{:S(2)}) %all-to-all-start) | async-done | bytes 32800 | tf_op jit(solution)/shard_map/all_to_all | solution.py:24
  36.7 0.6 broadcast.36
  37.3 0.8 reduce
  38.4 0.6 and.21
  39.1 5.5 %and.22 = pred[1024,4,288]{0,2,1:T(32,128)(4,1)S(1)} reshape(pred[16,64,4,16,18]{1,0,4,3,2:T(8,128)(4,1)S(1)} %and.21) | data formatting | bytes 2359296 | tf_op jit(solution)/shard_map/and | solution.py:29
  44.6 10.3 %all-gather.2.cloned.1.call-done = bf16[1024,2560]{1,0:T(8,128)(2,1)} async-done(((bf16[64,2560]{1,0:T(8,128)(2,1)}), bf16[1024,2560]{1,0:T(8,128)(2,1)}) %all-gather.2.cloned.1.call-update) | async-done | bytes 5242896 | tf_op jit(solution)/shard_map/all_gather | solution.py:17
  54.9 10.7 %convolution_convert_fusion = bf16[4,288,2560]{2,1,0:T(8,128)(2,1)} fusion(bf16[1024,2560]{1,0:T(8,128)(2,1)} %all-gather.2.cloned.1.call-done, pred[1024,4,288]{0,2,1:T(32,128)(4,1)S(1)} %and.22, pred[1024,288]{0,1:T(8,128)(4,1)} %and.24), kind=kOutput, calls=%fused_computation.10 | convolution fusion | flops 6043926528 | bytes 12615680 | tf_op jit(solution)/shard_map/ter,tm->erm/dot_general | solution.py:34
  65.5 29.0 %convolution_convert_fusion.1 = bf16[4,288,2560]{2,1,0:T(8,128)(2,1)} fusion(bf16[4,1536,2560]{2,1,0:T(8,128)(2,1)} %param.11, bf16[4,288,2560]{2,1,0:T(8,128)(2,1)} %convolution_convert_fusion, bf16[4,2560,1536]{2,1,0:T(8,128)(2,1)} %param.10), kind=kOutput, calls=%fused_computation.11 | convolution fusion | flops 18138267648 | bytes 74711040 | tf_op jit(solution)/shard_map/erf,efm->erm/dot_general | solution.py:36
  94.5 11.5 %convolution_bitcast_fusion = f32[1024,2560]{1,0:T(8,128)} fusion(bf16[4,288,2560]{2,1,0:T(8,128)(2,1)} %convolution_convert_fusion.1, pred[1024,4,288]{0,2,1:T(32,128)(4,1)S(1)} %and.22, bf16[1024,4]{0,1:T(4,128)(2,1)S(1)} %broadcast_in_dim.36, pred[1024,288]{0,1:T(8,128)(4,1)S(1)} %copy-done.1), kind=kOutput, calls=%fused_computation.9 | convolution fusion | flops 6042157056 | bytes 17866752 | tf_op jit(solution)/shard_map/ter,erm->tm/dot_general | solution.py:37
  106.1 66.7 %reduce-scatter.2.cloned.1.call-done = f32[64,2560]{1,0:T(8,128)} async-done(((f32[1024,2560]{1,0:T(8,128)}), f32[64,2560]{1,0:T(8,128)}) %reduce-scatter.2.cloned.1.call-update) | async-done | bytes 655376 | tf_op jit(solution)/shard_map/reduce_scatter | solution.py:38
  172.8 16.5 %fusion.15 = bf16[64,2560]{1,0:T(8,128)(2,1)} fusion(f32[64,2560]{1,0:T(8,128)} %reduce-scatter.2.cloned.1.call-done, bf16[3072,2560]{1,0:T(8,128)(2,1)} %param.13, bf16[64,2560]{1,0:T(8,128)(2,1)S(1)} %copy-done, bf16[2560,3072]{1,0:T(8,128)(2,1)} %param.12), kind=kOutput, calls=%fused_computation.20 | convolution fusion | flops 2015363072 | bytes 32768000 | tf_op jit(solution)/shard_map/dot_general | solution.py:40
  (20 shorter events, 0.7 us)
Async XLA Ops:
  6.5 48.3 %all-gather.2.cloned.1.call-start = ((), (), s32[]{:S(2)}) async-start(), calls=%async_computation.2 | async-start | bytes 5570560 | tf_op jit(solution)/shard_map/all_gather | solution.py:17
  18.7 18.1 %all-to-all-start = ((f32[16,1,512]{2,1,0:T(1,128)}), f32[16,1,512]{2,1,0:T(1,128)S(1)}, u32[]{:S(2)}, u32[]{:S(2)}) async-start(f32[16,1,512]{2,1,0:T(1,128)} %reshape.64), calls=%async_computation | async-start | bytes 65536 | tf_op jit(solution)/shard_map/all_to_all | solution.py:24
  29.4 143.4 %reduce-scatter.2.cloned.1.call-start = ((), (), s32[]{:S(2)}) async-start(), calls=%async_computation.3 | async-start | bytes 11141120 | tf_op jit(solution)/shard_map/reduce_scatter | solution.py:38
  65.5 29.0 %copy-start.1 = (pred[1024,288]{0,1:T(8,128)(4,1)S(1)}, pred[1024,288]{0,1:T(8,128)(4,1)}, u32[]{:S(2)}) copy-start(pred[1024,288]{0,1:T(8,128)(4,1)} %and.24) | copy-start | bytes 884740
  106.0 66.8 %copy-start = (bf16[64,2560]{1,0:T(8,128)(2,1)S(1)}, bf16[64,2560]{1,0:T(8,128)(2,1)}, u32[]{:S(2)}) copy-start(bf16[64,2560]{1,0:T(8,128)(2,1)} %param.7) | copy-start | bytes 983044
Sparse Core Ops, SparseCore 0:
  9.0 45.8 all-gather.1
  106.2 66.5 reduce-scatter.1

commit v2 on v0

v2 whole, which is shorter than its diff:
```python
import functools

import jax
import jax.numpy as jnp
from jax import lax
from jax.experimental import pallas as pl
from jax.experimental.pallas import tpu as pltpu
from jax.sharding import PartitionSpec as P

LOAD_MULT = 3
COLS = 256
LEAD = 3
CORES = 2
ABSENT = -4096.0
VMEM_BYTES = 67_000_000
F32 = jnp.float32
BF16 = jnp.bfloat16


def gelu(z):
    return 0.5 * z * (1.0 + jnp.tanh(0.7978845608028654 * (z + 0.044715 * (z * z * z))))


def moe_kernel(chips, cap, top_k,
               x_hbm, tab_hbm, wi_hbm, wo_hbm, si_hbm, so_hbm, y_ref,
               x_all, tabs, picks, codes, pick_mat, gate_mat, xg, hacc, h, outs, pbuf, ppush, prec, rbuf,
               sacc, s_act, u_all, wi_buf, wo_buf, si_buf, so_buf,
               ag_recv, tab_recv, ag_part, tab_part, ag_send, tab_send, own_sem,
               rs_recv, rs_send, pp_send, pp_recv, wi_sem, wo_sem, si_sem, so_sem):
    rows, d_model = x_hbm.shape
    experts = wi_hbm.shape[0]
    nc = d_model // COLS
    hops = chips // 2
    half = rows // 2
    group_rows = chips * rows
    slots = chips * cap

    ep = lax.axis_index('ep')
    z, c = ep // CORES, ep % CORES
    partner = {'ep': z * CORES + (1 - c)}
    nxt = {'ep': ((z + 1) % chips) * CORES + c}
    prv = {'ep': ((z + chips - 1) % chips) * CORES + c}

    def chip(off):
        return (z + off + chips) % chips

    def xrows(w, s, lo=0, count=None):
        base = (c * chips + s) * rows + lo
        return x_all.at[w, pl.ds(pl.multiple_of(base, half), rows if count is None else count)]

    def tblk(s, lo=0, count=None):
        t = tabs.at[c * chips + s]
        return t if count is None else t.at[pl.ds(lo, count)]

    def remote(src, dst, ssem, rsem, dev):
        return pltpu.make_async_remote_copy(src_ref=src, dst_ref=dst, send_sem=ssem, recv_sem=rsem, device_id=dev, device_id_type=pl.DeviceIdType.MESH)

    def ag_copy(w, k, up):
        s = chip(-(k - 1)) if up else chip(k - 1)
        lo, cnt = (0, None) if k < hops else ((0, half) if up else (half, half))
        ref = xrows(w, s, lo, cnt)
        return remote(ref, ref, ag_send.at[w], ag_recv.at[0 if up else 1, w, k - 1], nxt if up else prv)

    def ag_arrival(w, k, up):
        s = chip(-k) if up else chip(k)
        lo, cnt = (0, None) if k < hops else ((0, half) if up else (half, half))
        ref = xrows(w, s, lo, cnt)
        return remote(ref, ref, ag_send.at[w], ag_recv.at[0 if up else 1, w, k - 1], nxt if up else prv)

    def tab_copy(k, up, arrival):
        off = k if arrival else k - 1
        s = chip(-off) if up else chip(off)
        lo, cnt = (0, None) if k < hops else ((0, 8) if up else (8, 8))
        ref = tblk(s, lo, cnt)
        return remote(ref, ref, tab_send, tab_recv.at[0 if up else 1, k - 1], nxt if up else prv)

    def ag_push(w, s):
        ref = xrows(w, s)
        return remote(ref, ref, ag_send.at[w], ag_part.at[w], partner)

    def tab_push(s):
        ref = tblk(s)
        return remote(ref, ref, tab_send, tab_part, partner)

    def wi_copy(w):
        return pltpu.make_async_copy(wi_hbm.at[:, pl.ds(pl.multiple_of(w * COLS, COLS), COLS), :], wi_buf.at[w % 2], wi_sem.at[w % 2])

    def wo_copy(w):
        return pltpu.make_async_copy(wo_hbm.at[:, :, pl.ds(pl.multiple_of(w * COLS, COLS), COLS)], wo_buf.at[w % 2], wo_sem.at[w % 2])

    def si_copy(w):
        return pltpu.make_async_copy(si_hbm.at[pl.ds(pl.multiple_of(w * COLS, COLS), COLS), :], si_buf.at[w % 2], si_sem.at[w % 2])

    def so_copy(w):
        return pltpu.make_async_copy(so_hbm.at[:, pl.ds(pl.multiple_of(w * COLS, COLS), COLS)], so_buf.at[w % 2], so_sem.at[w % 2])

    for w in range(nc):
        pltpu.make_async_copy(x_hbm.at[:, pl.ds(w * COLS, COLS)], xrows(w, z), own_sem.at[0]).start()
    pltpu.make_async_copy(tab_hbm, tblk(z), own_sem.at[1]).start()
    for w in range(2):
        si_copy(w).start()
    for w in range(2):
        wi_copy(w).start()

    barrier = pltpu.get_barrier_semaphore()
    for dev in (nxt, prv, partner):
        pl.semaphore_signal(barrier, inc=1, device_id=dev, device_id_type=pl.DeviceIdType.MESH)
    pl.semaphore_wait(barrier, 3)

    pltpu.make_async_copy(tab_hbm, tblk(z), own_sem.at[1]).wait()
    own_all = x_all.at[0, pl.ds(0, nc * rows)]
    pltpu.make_async_copy(own_all, own_all, own_sem.at[0]).wait()
    tab_copy(1, True, False).start()
    tab_copy(1, False, False).start()
    tab_push(z).start()
    for w in range(min(LEAD, nc)):
        ag_copy(w, 1, True).start()
        ag_copy(w, 1, False).start()
        ag_push(w, z).start()
    for w in range(2):
        wo_copy(w).start()
        so_copy(w).start()

    def build_tables():
        base = (ep * experts).astype(F32)
        lane = lax.broadcasted_iota(jnp.int32, (1, 2 * rows), 1)
        pairs = chips // 2
        for g in range(2):
            cc = c if g == 0 else 1 - c
            for i in range(pairs):
                t = tabs[cc * chips + 2 * i] + tabs[cc * chips + 2 * i + 1]
                ids, gts = t[0:top_k], t[8:8 + top_k]
                for e in range(experts):
                    hit = ids == (base + float(e))
                    r = (g * pairs + i) * experts + e
                    picks[r:r + 1, :] = jnp.sum(hit.astype(F32), axis=0, keepdims=True)
                    codes[g, experts + e:experts + e + 1, i * 2 * rows:(i + 1) * 2 * rows] = jnp.sum(jnp.where(hit, gts, 0.0), axis=0, keepdims=True)
        a = lax.broadcasted_iota(jnp.int32, (2 * rows, 2 * rows), 0)
        b = lax.broadcasted_iota(jnp.int32, (2 * rows, 2 * rows), 1)
        before = ((a < b) & ((a >= rows) == (b >= rows))).astype(F32).astype(BF16)
        rank = jnp.dot(picks[...].astype(BF16), before, preferred_element_type=F32)
        for g in range(2):
            for i in range(pairs):
                start = (2 * i * cap + jnp.where(lane >= rows, cap, 0)).astype(F32)
                for e in range(experts):
                    r = (g * pairs + i) * experts + e
                    code = jnp.where(picks[r:r + 1, :] > 0.5, rank[r:r + 1, :] + start, ABSENT)
                    codes[g, e:e + 1, i * 2 * rows:(i + 1) * 2 * rows] = code
        slot = lax.broadcasted_iota(jnp.int32, (slots, group_rows), 0).astype(F32)
        col = lax.broadcasted_iota(jnp.int32, (2 * rows, experts * slots), 1).astype(F32)
        for g in range(2):
            for e in range(experts):
                pick_mat[g, e * slots:(e + 1) * slots, :] = jnp.where(slot == codes[g, e:e + 1, :], 1.0, 0.0).astype(BF16)
            for i in range(pairs):
                ct = jnp.transpose(codes[g, :, i * 2 * rows:(i + 1) * 2 * rows])
                acc = jnp.zeros((2 * rows, experts * slots), F32)
                for e in range(experts):
                    acc = jnp.where(col == ct[:, e:e + 1] + float(e * slots), ct[:, experts + e:experts + e + 1], acc)
                gate_mat[g, i * 2 * rows:(i + 1) * 2 * rows, :] = acc.astype(BF16)

    def gather(w, g):
        cc = c if g == 0 else 1 - c
        xs = x_all[w, pl.ds(pl.multiple_of(cc * group_rows, group_rows), group_rows), :]
        got = jnp.dot(pick_mat[g], xs, preferred_element_type=F32).astype(BF16)
        for e in range(experts):
            xg[e, g * slots:(g + 1) * slots, :] = got[e * slots:(e + 1) * slots, :]

    def in_step(j, carry):
        w = j + LEAD

        @pl.when(w < nc)
        def _():
            ag_copy(w, 1, True).start()
            ag_copy(w, 1, False).start()
            ag_push(w, z).start()

        for k in range(1, hops):
            w = j - (k - 1)

            @pl.when((w >= 0) & (w < nc))
            def _():
                if k >= 1:
                    @pl.when(w == 0)
                    def _():
                        for up in (True, False):
                            tab_copy(k, up, True).wait_recv()
                            tab_copy(k + 1, up, False).start()
                        tab_push(chip(-k)).start()
                        tab_push(chip(k)).start()
                for up in (True, False):
                    ag_arrival(w, k, up).wait_recv()
                    ag_copy(w, k + 1, up).start()
                ag_push(w, chip(-k)).start()
                ag_push(w, chip(k)).start()

        w = j - (hops - 1)

        @pl.when((w >= 0) & (w < nc))
        def _():
            for up in (True, False):
                ag_arrival(w, hops, up).wait_recv()
            ag_push(w, chip(hops)).start()

            @pl.when(w == 0)
            def _():
                for up in (True, False):
                    tab_copy(hops, up, True).wait_recv()
                tab_push(chip(hops)).start()

        @pl.when(j < nc)
        def _():
            si_copy(j).wait()
            mine = x_all[j, pl.ds(pl.multiple_of((c * chips + z) * rows, rows), rows), :]
            part = jnp.dot(mine, si_buf[j % 2], preferred_element_type=F32)

            @pl.when(j == 0)
            def _():
                sacc[...] = part

            @pl.when(j > 0)
            def _():
                sacc[...] += part

            @pl.when(j + 2 < nc)
            def _():
                si_copy(j + 2).start()

        @pl.when((w >= 0) & (w < nc))
        def _():
            @pl.when(w == 0)
            def _():
                theirs = tabs.at[pl.ds((1 - c) * chips, chips)]
                pltpu.make_async_copy(theirs, theirs, tab_part).wait()
                build_tables()

            gather(w, 0)
            theirs = x_all.at[w, pl.ds(pl.multiple_of((1 - c) * group_rows, group_rows), group_rows)]
            pltpu.make_async_copy(theirs, theirs, ag_part.at[w]).wait()
            gather(w, 1)
            wi_copy(w).wait()

            @pl.when(w == 0)
            def _():
                hacc[...] = jnp.zeros_like(hacc)

            for e in range(experts):
                hacc[e] += jnp.dot(xg[e], wi_buf[w % 2, e], preferred_element_type=F32)

            @pl.when(w + 2 < nc)
            def _():
                wi_copy(w + 2).start()

        return carry

    lax.fori_loop(0, nc + hops - 1, in_step, 0)

    def act_step(e, carry):
        h[e] = gelu(hacc[e]).astype(BF16)
        return carry

    lax.fori_loop(0, experts, act_step, 0)
    s_act[...] = gelu(sacc[...]).astype(BF16)

    def prow(w, s, lo=0, count=None):
        return pbuf.at[w, pl.ds(pl.multiple_of(s * rows + lo, half), rows if count is None else count)]

    def rs_copy(w, k, up):
        off = hops - k + 1
        s = chip(off) if up else chip(-off)
        lo, cnt = (0, rows) if k > 1 else ((0, half) if up else (half, half))
        d = 0 if up else 1
        return remote(prow(w, s, lo, cnt), rbuf.at[d, w, k - 1, pl.ds(lo, cnt)], rs_send.at[w], rs_recv.at[d, w, k - 1], nxt if up else prv)

    def push_copy(w):
        return remote(ppush.at[w % 2], prec.at[w % 2], pp_send.at[w % 2], pp_recv.at[w % 2], partner)

    def out_step(i, carry):
        @pl.when(i < nc)
        def _():
            wo_copy(i).wait()
            for e in range(experts):
                o = jnp.dot(h[e], wo_buf[i % 2, e], preferred_element_type=F32).astype(BF16)
                outs[0, e * slots:(e + 1) * slots, :] = o[:slots]
                outs[1, e * slots:(e + 1) * slots, :] = o[slots:]

            @pl.when(i >= 2)
            def _():
                push_copy(i).wait_send()

            ppush[i % 2] = jnp.dot(gate_mat[1], outs[1], preferred_element_type=F32)
            push_copy(i).start()
            pbuf[i] = jnp.dot(gate_mat[0], outs[0], preferred_element_type=F32)
            so_copy(i).wait()
            u_all[i] = jnp.dot(s_act[...], so_buf[i % 2], preferred_element_type=F32)

            @pl.when(i + 2 < nc)
            def _():
                wo_copy(i + 2).start()
                so_copy(i + 2).start()

            push_copy(i).wait_recv()
            pbuf[i] += prec[i % 2]
            rs_copy(i, 1, True).start()
            rs_copy(i, 1, False).start()

        for k in range(hops - 1, 0, -1):
            w = i - k

            @pl.when((w >= 0) & (w < nc))
            def _():
                for up in (True, False):
                    rs_copy(w, k, up).wait_recv()
                    d = 0 if up else 1
                    s = chip(hops - k) if up else chip(-(hops - k))
                    lo, cnt = (0, rows) if k > 1 else ((0, half) if up else (half, half))
                    dst = prow(w, s, lo, cnt)
                    dst[...] += rbuf[d, w, k - 1, lo:lo + cnt, :]
                    rs_copy(w, k + 1, up).start()

        w = i - hops

        @pl.when(w >= 0)
        def _():
            rs_copy(w, hops, True).wait_recv()
            rs_copy(w, hops, False).wait_recv()
            total = prow(w, z)[...] + (rbuf[0, w, hops - 1] + rbuf[1, w, hops - 1]) + u_all[w]
            y_ref[:, pl.ds(pl.multiple_of(w * COLS, COLS), COLS)] = total.astype(BF16)

        return carry

    lax.fori_loop(0, nc + hops, out_step, 0)

    def drain(w, carry):
        sent = x_all.at[w, pl.ds(0, (2 * chips - 1) * rows)]
        pltpu.make_async_copy(sent, sent, ag_send.at[w]).wait()
        sums = pbuf.at[w, pl.ds(0, (chips - 1) * rows)]
        pltpu.make_async_copy(sums, sums, rs_send.at[w]).wait()
        return carry

    lax.fori_loop(0, nc, drain, 0)
    sent = tabs.at[pl.ds(0, 2 * chips - 1)]
    pltpu.make_async_copy(sent, sent, tab_send).wait()
    for w in range(min(2, nc)):
        push_copy(w).wait_send()


def solution(mesh):
    group_size = mesh.shape['ep']
    chips = group_size // CORES
    hops = chips // 2

    def local_layer(x_loc, idx_loc, gate_loc, w_in, w_out, shared_in, shared_out):
        rows, top_k = idx_loc.shape
        d_model = x_loc.shape[1]
        experts, _, ff = w_in.shape
        fs = shared_in.shape[1]
        num_experts = experts * group_size
        cap = min(rows, LOAD_MULT * rows * top_k // num_experts)
        slots = chips * cap
        nc = d_model // COLS
        parity = (lax.axis_index('ep') // CORES) % 2
        pad = jnp.zeros((8 - top_k, rows), F32)
        tab = jnp.concatenate([idx_loc.T.astype(F32), pad, gate_loc.T, pad], axis=0)
        side = (jnp.arange(2 * rows)[None, :] >= rows) == (parity == 1)
        tab = jnp.where(side, jnp.concatenate([tab, tab], axis=1), 0.0)
        any_spec = pl.BlockSpec(memory_space=pl.ANY)
        dma = pltpu.SemaphoreType.DMA
        flops = 2 * group_size * cap * experts * d_model * ff * 2
        return pl.pallas_call(
            functools.partial(moe_kernel, chips, cap, top_k),
            out_shape=jax.ShapeDtypeStruct((rows, d_model), BF16),
            in_specs=[any_spec] * 6,
            out_specs=pl.BlockSpec(memory_space=pltpu.VMEM),
            scratch_shapes=[
                pltpu.VMEM((nc, group_size * rows, COLS), BF16),
                pltpu.VMEM((group_size, 16, 2 * rows), F32),
                pltpu.VMEM((chips * experts, 2 * rows), F32),
                pltpu.VMEM((2, 2 * experts, chips * rows), F32),
                pltpu.VMEM((2, experts * slots, chips * rows), BF16),
                pltpu.VMEM((2, chips * rows, experts * slots), BF16),
                pltpu.VMEM((experts, 2 * slots, COLS), BF16),
                pltpu.VMEM((experts, 2 * slots, ff), F32),
                pltpu.VMEM((experts, 2 * slots, ff), BF16),
                pltpu.VMEM((2, experts * slots, COLS), BF16),
                pltpu.VMEM((nc, chips * rows, COLS), F32),
                pltpu.VMEM((2, chips * rows, COLS), F32),
                pltpu.VMEM((2, chips * rows, COLS), F32),
                pltpu.VMEM((2, nc, hops, rows, COLS), F32),
                pltpu.VMEM((rows, fs), F32),
                pltpu.VMEM((rows, fs), BF16),
                pltpu.VMEM((nc, rows, COLS), F32),
                pltpu.VMEM((2, experts, COLS, ff), BF16),
                pltpu.VMEM((2, experts, ff, COLS), BF16),
                pltpu.VMEM((2, COLS, fs), BF16),
                pltpu.VMEM((2, fs, COLS), BF16),
                dma((2, nc, hops)), dma((2, hops)), dma((nc,)), dma(()), dma((nc,)), dma(()), dma((2,)),
                dma((2, nc, hops)), dma((nc,)), dma((2,)), dma((2,)),
                dma((2,)), dma((2,)), dma((2,)), dma((2,)),
            ],
            compiler_params=pltpu.CompilerParams(collective_id=0, has_side_effects=True, vmem_limit_bytes=VMEM_BYTES),
            cost_estimate=pl.CostEstimate(flops=flops, bytes_accessed=2 * (w_in.size + w_out.size + shared_in.size + shared_out.size), transcendentals=0),
        )(x_loc, tab, w_in, w_out, shared_in, shared_out)

    tok_spec = P(('dp', 'ep'), None)
    expert_spec = P('ep', None, None)
    whole_spec = P(None, None)
    return jax.shard_map(local_layer, mesh=mesh, in_specs=(tok_spec, tok_spec, tok_spec, expert_spec, expert_spec, whole_spec, whole_spec), out_specs=tok_spec, check_vma=False)
```

time: 419 us -> 134 us (0.32)
  blocking collectives: 319 us -> 0 us
  Pallas kernels: 0 us -> 129 us
  matrix products: 55.5 us -> 0 us
  local copies, waits for them, and re-layouts: 41.9 us -> 1.72 us
    all_to_all x2 -> x0, blocking collectives: 319 us -> none  [the longest x1 184 us: local_layer(): recv_rows = lax.all_to_all(send_rows, 'ep', 0, 1, tiled=True)]
    pallas_call x0 -> x1, Pallas kernels: none -> 129 us  [local_layer(): pl.pallas_call(functools.partial(moe_kernel, chips, cap, top_k), out_shap...]
    dot_general x5 -> x0, matrix products: 55.5 us -> none  [the longest x1 30.2 us: local_layer(): jnp.einsum('erf,efm->erm', hidden, w_out, preferred_element_type=jnp.floa...]
    all_to_all x3 -> x0, local copies, waits for them, and re-layouts: 27.1 us -> none  [the longest x2 18.3 us: local_layer(): back_rows = lax.all_to_all(expert_out, 'ep', 1, 0, tiled=True)]
    convert_element_type x3 -> x0, local copies, waits for them, and re-layouts: 13.3 us -> none  [the longest x1 7.22 us: local_layer(): jnp.einsum('erf,efm->erm', hidden, w_out, preferred_element_type=jnp.floa...]
where the time goes in v2:
time: 134 us; the launch traced here: 133 us
  Pallas kernels  129 us (96%)
  other arithmetic  2.14 us (2%)
  local copies, waits for them, and re-layouts  1.72 us (1%)
    pallas_call x1, Pallas kernels, local_layer(): pl.pallas_call(functools.partial(moe_kernel, chips, cap, top_k), out_shap...  129 us

profile of v2, /device:TPU:21, one launch (start us, length us, event | category | flops | bytes accessed | tf_op | source)
XLA Modules:
  0.0 133.0 jit_solution(6728754434468589810)
XLA Ops:
  0.0 0.7 convert_bitcast_fusion
  0.7 1.4 %maximum_select_fusion.tab_hbm = f32[16,128]{1,0:T(8,128)} fusion(f32[2,64]{1,0:T(2,128)S(1)} %broadcast_in_dim.17, f32[6,64]{1,0:T(8,128)} %bitcast.3, f32[6,64]{1,0:T(8,128)S(1)} %convert_bitcast_fusion, pred[128]{0:T(512)(128)(4,1)S(1)} %compare_compare_fusion), kind=kLoop, calls=%fused_computation | loop fusion | flops 16384 | bytes 11904 | tf_op jit(solution)/shard_map/jit(_where)/select_n | solution.py:365
  2.1 129.1 %shard_map.73 = bf16[64,2560]{1,0:T(8,128)(2,1)} custom-call(bf16[64,2560]{1,0:T(8,128)(2,1)} %x_hbm.1, f32[16,128]{1,0:T(8,128)} %maximum_select_fusion.tab_hbm, bf16[4,2560,1536]{2,1,0:T(8,128)(2,1)} %wi_hbm.1, bf16[4,1536,2560]{2,1,0:T(8,128)(2,1)} %wo_hbm.1, bf16[2560,3072]{1,0:T(8,128)(2,1)} %si_hbm.1, bf16[3072,2560]{1,0:T(8,128)(2,1)} %so_hbm.1), custom_call_target="tpu_custom_call" | custom-call | flops 18119393280 | bytes 94371840 | tf_op jit(solution)/shard_map/pallas_call | solution.py:369
  131.3 1.7 %copy.9 = bf16[64,2560]{1,0:T(8,128)(2,1)} copy(bf16[64,2560]{1,0:T(8,128)(2,1)} %shard_map.73) | data formatting | bytes 655360
  (2 shorter events, 0.0 us)

commit v3 on v2

--- a/solution.py
+++ b/solution.py
@@ -9,7 +9,10 @@
 
 LOAD_MULT = 3
 COLS = 256
-LEAD = 3
+LEAD = 4
+AG_LAG = 2
+RS_LAG = 2
+PAIR = 2
 CORES = 2
 ABSENT = -4096.0
 VMEM_BYTES = 67_000_000
@@ -22,8 +25,8 @@
 
 
 def moe_kernel(chips, cap, top_k,
-               x_hbm, tab_hbm, wi_hbm, wo_hbm, si_hbm, so_hbm, y_ref,
-               x_all, tabs, picks, codes, pick_mat, gate_mat, xg, hacc, h, outs, pbuf, ppush, prec, rbuf,
+               x_hbm, idx_hbm, top_hbm, wi_hbm, wo_hbm, si_hbm, so_hbm, y_ref,
+               x_all, idx_v, top_v, tabs, picks, codes, pick_mat, gate_mat, xg, hacc, h, outs, pbuf, ppush, prec, rbuf,
                sacc, s_act, u_all, wi_buf, wo_buf, si_buf, so_buf,
                ag_recv, tab_recv, ag_part, tab_part, ag_send, tab_send, own_sem,
                rs_recv, rs_send, pp_send, pp_recv, wi_sem, wo_sem, si_sem, so_sem):
@@ -37,12 +40,14 @@
 
     ep = lax.axis_index('ep')
     z, c = ep // CORES, ep % CORES
-    partner = {'ep': z * CORES + (1 - c)}
-    nxt = {'ep': ((z + 1) % chips) * CORES + c}
-    prv = {'ep': ((z + chips - 1) % chips) * CORES + c}
+    first = lax.axis_index('dp') * (chips * CORES)
+    partner = first + z * CORES + (1 - c)
+    nxt = first + ((z + 1) % chips) * CORES + c
+    prv = first + ((z + chips - 1) % chips) * CORES + c
+    near = [(z + off) % chips for off in range(chips)]
 
     def chip(off):
-        return (z + off + chips) % chips
+        return near[off % chips]
 
     def xrows(w, s, lo=0, count=None):
         base = (c * chips + s) * rows + lo
@@ -53,7 +58,7 @@
         return t if count is None else t.at[pl.ds(lo, count)]
 
     def remote(src, dst, ssem, rsem, dev):
-        return pltpu.make_async_remote_copy(src_ref=src, dst_ref=dst, send_sem=ssem, recv_sem=rsem, device_id=dev, device_id_type=pl.DeviceIdType.MESH)
+        return pltpu.make_async_remote_copy(src_ref=src, dst_ref=dst, send_sem=ssem, recv_sem=rsem, device_id=dev, device_id_type=pl.DeviceIdType.LOGICAL)
 
     def ag_copy(w, k, up):
         s = chip(-(k - 1)) if up else chip(k - 1)
@@ -83,7 +88,7 @@
         return remote(ref, ref, tab_send, tab_part, partner)
 
     def wi_copy(w):
-        return pltpu.make_async_copy(wi_hbm.at[:, pl.ds(pl.multiple_of(w * COLS, COLS), COLS), :], wi_buf.at[w % 2], wi_sem.at[w % 2])
+        return pltpu.make_async_copy(wi_hbm.at[:, pl.ds(pl.multiple_of(w * PAIR * COLS, COLS), PAIR * COLS), :], wi_buf.at[w % 2], wi_sem.at[w % 2])
 
     def wo_copy(w):
         return pltpu.make_async_copy(wo_hbm.at[:, :, pl.ds(pl.multiple_of(w * COLS, COLS), COLS)], wo_buf.at[w % 2], wo_sem.at[w % 2])
@@ -96,7 +101,8 @@
 
     for w in range(nc):
         pltpu.make_async_copy(x_hbm.at[:, pl.ds(w * COLS, COLS)], xrows(w, z), own_sem.at[0]).start()
-    pltpu.make_async_copy(tab_hbm, tblk(z), own_sem.at[1]).start()
+    pltpu.make_async_copy(idx_hbm, idx_v, own_sem.at[1]).start()
+    pltpu.make_async_copy(top_hbm, top_v, own_sem.at[2]).start()
     for w in range(2):
         si_copy(w).start()
     for w in range(2):
@@ -104,22 +110,33 @@
 
     barrier = pltpu.get_barrier_semaphore()
     for dev in (nxt, prv, partner):
-        pl.semaphore_signal(barrier, inc=1, device_id=dev, device_id_type=pl.DeviceIdType.MESH)
+        pl.semaphore_signal(barrier, inc=1, device_id=dev, device_id_type=pl.DeviceIdType.LOGICAL)
     pl.semaphore_wait(barrier, 3)
 
-    pltpu.make_async_copy(tab_hbm, tblk(z), own_sem.at[1]).wait()
+    pltpu.make_async_copy(idx_hbm, idx_v, own_sem.at[1]).wait()
+    pltpu.make_async_copy(top_hbm, top_v, own_sem.at[2]).wait()
+    right = lax.broadcasted_iota(jnp.int32, (top_k, 2 * rows), 1) >= rows
+    side = right == (z % 2 == 1)
+    ids, gts = idx_v[...].astype(F32), top_v[...]
+    mine = tabs.at[c * chips + z]
+    mine[...] = jnp.zeros_like(mine)
+    mine[0:top_k, :] = jnp.where(side, jnp.concatenate([ids, ids], axis=1), 0.0)
+    mine[8:8 + top_k, :] = jnp.where(side, jnp.concatenate([gts, gts], axis=1), 0.0)
     own_all = x_all.at[0, pl.ds(0, nc * rows)]
     pltpu.make_async_copy(own_all, own_all, own_sem.at[0]).wait()
-    tab_copy(1, True, False).start()
-    tab_copy(1, False, False).start()
-    tab_push(z).start()
     for w in range(min(LEAD, nc)):
         ag_copy(w, 1, True).start()
         ag_copy(w, 1, False).start()
+        if w == 0:
+            tab_copy(1, True, False).start()
+            tab_copy(1, False, False).start()
+            tab_push(z).start()
         ag_push(w, z).start()
     for w in range(2):
         wo_copy(w).start()
         so_copy(w).start()
+
+    hacc[...] = jnp.zeros_like(hacc)
 
     def build_tables():
         base = (ep * experts).astype(F32)
@@ -158,42 +175,65 @@
                     acc = jnp.where(col == ct[:, e:e + 1] + float(e * slots), ct[:, experts + e:experts + e + 1], acc)
                 gate_mat[g, i * 2 * rows:(i + 1) * 2 * rows, :] = acc.astype(BF16)
 
-    def gather(w, g):
+    def gather(w, g, part):
         cc = c if g == 0 else 1 - c
         xs = x_all[w, pl.ds(pl.multiple_of(cc * group_rows, group_rows), group_rows), :]
         got = jnp.dot(pick_mat[g], xs, preferred_element_type=F32).astype(BF16)
         for e in range(experts):
-            xg[e, g * slots:(g + 1) * slots, :] = got[e * slots:(e + 1) * slots, :]
+            xg[e, g * slots:(g + 1) * slots, part * COLS:(part + 1) * COLS] = got[e * slots:(e + 1) * slots, :]
+
+    ag_span = (hops - 1) * AG_LAG
 
     def in_step(j, carry):
-        w = j + LEAD
-
-        @pl.when(w < nc)
-        def _():
-            ag_copy(w, 1, True).start()
-            ag_copy(w, 1, False).start()
-            ag_push(w, z).start()
-
-        for k in range(1, hops):
-            w = j - (k - 1)
+        for k in range(hops - 1, 0, -1):
+            w = j - (k - 1) * AG_LAG
 
             @pl.when((w >= 0) & (w < nc))
             def _():
-                if k >= 1:
-                    @pl.when(w == 0)
-                    def _():
-                        for up in (True, False):
-                            tab_copy(k, up, True).wait_recv()
-                            tab_copy(k + 1, up, False).start()
-                        tab_push(chip(-k)).start()
-                        tab_push(chip(k)).start()
                 for up in (True, False):
                     ag_arrival(w, k, up).wait_recv()
                     ag_copy(w, k + 1, up).start()
                 ag_push(w, chip(-k)).start()
                 ag_push(w, chip(k)).start()
 
-        w = j - (hops - 1)
+                @pl.when(w == 0)
+                def _():
+                    for up in (True, False):
+                        tab_copy(k, up, True).wait_recv()
+                        tab_copy(k + 1, up, False).start()
+                    tab_push(chip(-k)).start()
+                    tab_push(chip(k)).start()
+
+        w = j + LEAD
+
+        @pl.when(w < nc)
+        def _():
+            ag_copy(w, 1, True).start()
+            ag_copy(w, 1, False).start()
+            ag_push(w, z).start()
+
+        for q in range(2):
+            v = 2 * j + q
+
+            @pl.when(v < nc)
+            def _():
+                si_copy(v).wait()
+                mine = x_all[v, pl.ds(pl.multiple_of((c * chips + z) * rows, rows), rows), :]
+                part = jnp.dot(mine, si_buf[v % 2], preferred_element_type=F32)
+
+                @pl.when(v == 0)
+                def _():
+                    sacc[...] = part
+
+                @pl.when(v > 0)
+                def _():
+                    sacc[...] += part
+
+                @pl.when(v + 2 < nc)
+                def _():
+                    si_copy(v + 2).start()
+
+        w = j - ag_span
 
         @pl.when((w >= 0) & (w < nc))
         def _():
@@ -206,59 +246,40 @@
                 for up in (True, False):
                     tab_copy(hops, up, True).wait_recv()
                 tab_push(chip(hops)).start()
-
-        @pl.when(j < nc)
-        def _():
-            si_copy(j).wait()
-            mine = x_all[j, pl.ds(pl.multiple_of((c * chips + z) * rows, rows), rows), :]
-            part = jnp.dot(mine, si_buf[j % 2], preferred_element_type=F32)
-
-            @pl.when(j == 0)
-            def _():
-                sacc[...] = part
-
-            @pl.when(j > 0)
-            def _():
-                sacc[...] += part
-
-            @pl.when(j + 2 < nc)
-            def _():
-                si_copy(j + 2).start()
-
-        @pl.when((w >= 0) & (w < nc))
-        def _():
-            @pl.when(w == 0)
-            def _():
                 theirs = tabs.at[pl.ds((1 - c) * chips, chips)]
                 pltpu.make_async_copy(theirs, theirs, tab_part).wait()
                 build_tables()
 
-            gather(w, 0)
-            theirs = x_all.at[w, pl.ds(pl.multiple_of((1 - c) * group_rows, group_rows), group_rows)]
-            pltpu.make_async_copy(theirs, theirs, ag_part.at[w]).wait()
-            gather(w, 1)
-            wi_copy(w).wait()
-
-            @pl.when(w == 0)
-            def _():
-                hacc[...] = jnp.zeros_like(hacc)
-
-            for e in range(experts):
-                hacc[e] += jnp.dot(xg[e], wi_buf[w % 2, e], preferred_element_type=F32)
-
-            @pl.when(w + 2 < nc)
-            def _():
-                wi_copy(w + 2).start()
+        @pl.when((w >= 0) & (w < nc) & (w % PAIR == PAIR - 1))
+        def _():
+            m = w // PAIR
+            for part in range(PAIR):
+                gather(m * PAIR + part, 0, part)
+            for part in range(PAIR):
+                v = m * PAIR + part
+                theirs = x_all.at[v, pl.ds(pl.multiple_of((1 - c) * group_rows, group_rows), group_rows)]
+                pltpu.make_async_copy(theirs, theirs, ag_part.at[v]).wait()
+                gather(v, 1, part)
+            wi_copy(m).wait()
+
+            @pl.when(w < nc - 1)
+            def _():
+                for e in range(experts):
+                    hacc[e] += jnp.dot(xg[e], wi_buf[m % 2, e], preferred_element_type=F32)
+
+            @pl.when(w == nc - 1)
+            def _():
+                for e in range(experts):
+                    h[e] = gelu(hacc[e] + jnp.dot(xg[e], wi_buf[m % 2, e], preferred_element_type=F32)).astype(BF16)
+
+            @pl.when(m + 2 < nc // PAIR)
+            def _():
+                wi_copy(m + 2).start()
 
         return carry
 
-    lax.fori_loop(0, nc + hops - 1, in_step, 0)
-
-    def act_step(e, carry):
-        h[e] = gelu(hacc[e]).astype(BF16)
-        return carry
-
-    lax.fori_loop(0, experts, act_step, 0)
+    lax.fori_loop(0, nc + ag_span, in_step, 0)
+
     s_act[...] = gelu(sacc[...]).astype(BF16)
 
     def prow(w, s, lo=0, count=None):
@@ -298,13 +319,8 @@
                 wo_copy(i + 2).start()
                 so_copy(i + 2).start()
 
-            push_copy(i).wait_recv()
-            pbuf[i] += prec[i % 2]
-            rs_copy(i, 1, True).start()
-            rs_copy(i, 1, False).start()
-
         for k in range(hops - 1, 0, -1):
-            w = i - k
+            w = i - k * RS_LAG
 
             @pl.when((w >= 0) & (w < nc))
             def _():
@@ -317,7 +333,14 @@
                     dst[...] += rbuf[d, w, k - 1, lo:lo + cnt, :]
                     rs_copy(w, k + 1, up).start()
 
-        w = i - hops
+        @pl.when(i < nc)
+        def _():
+            push_copy(i).wait_recv()
+            pbuf[i] += prec[i % 2]
+            rs_copy(i, 1, True).start()
+            rs_copy(i, 1, False).start()
+
+        w = i - hops * RS_LAG
 
         @pl.when(w >= 0)
         def _():
@@ -328,7 +351,7 @@
 
         return carry
 
-    lax.fori_loop(0, nc + hops, out_step, 0)
+    lax.fori_loop(0, nc + hops * RS_LAG, out_step, 0)
 
     def drain(w, carry):
         sent = x_all.at[w, pl.ds(0, (2 * chips - 1) * rows)]
@@ -358,27 +381,24 @@
         cap = min(rows, LOAD_MULT * rows * top_k // num_experts)
         slots = chips * cap
         nc = d_model // COLS
-        parity = (lax.axis_index('ep') // CORES) % 2
-        pad = jnp.zeros((8 - top_k, rows), F32)
-        tab = jnp.concatenate([idx_loc.T.astype(F32), pad, gate_loc.T, pad], axis=0)
-        side = (jnp.arange(2 * rows)[None, :] >= rows) == (parity == 1)
-        tab = jnp.where(side, jnp.concatenate([tab, tab], axis=1), 0.0)
         any_spec = pl.BlockSpec(memory_space=pl.ANY)
         dma = pltpu.SemaphoreType.DMA
         flops = 2 * group_size * cap * experts * d_model * ff * 2
         return pl.pallas_call(
             functools.partial(moe_kernel, chips, cap, top_k),
             out_shape=jax.ShapeDtypeStruct((rows, d_model), BF16),
-            in_specs=[any_spec] * 6,
+            in_specs=[any_spec] * 7,
             out_specs=pl.BlockSpec(memory_space=pltpu.VMEM),
             scratch_shapes=[
                 pltpu.VMEM((nc, group_size * rows, COLS), BF16),
+                pltpu.VMEM((top_k, rows), jnp.int32),
+                pltpu.VMEM((top_k, rows), F32),
                 pltpu.VMEM((group_size, 16, 2 * rows), F32),
                 pltpu.VMEM((chips * experts, 2 * rows), F32),
                 pltpu.VMEM((2, 2 * experts, chips * rows), F32),
                 pltpu.VMEM((2, experts * slots, chips * rows), BF16),
                 pltpu.VMEM((2, chips * rows, experts * slots), BF16),
-                pltpu.VMEM((experts, 2 * slots, COLS), BF16),
+                pltpu.VMEM((experts, 2 * slots, PAIR * COLS), BF16),
                 pltpu.VMEM((experts, 2 * slots, ff), F32),
                 pltpu.VMEM((experts, 2 * slots, ff), BF16),
                 pltpu.VMEM((2, experts * slots, COLS), BF16),
@@ -389,17 +409,17 @@
                 pltpu.VMEM((rows, fs), F32),
                 pltpu.VMEM((rows, fs), BF16),
                 pltpu.VMEM((nc, rows, COLS), F32),
-                pltpu.VMEM((2, experts, COLS, ff), BF16),
+                pltpu.VMEM((2, experts, PAIR * COLS, ff), BF16),
                 pltpu.VMEM((2, experts, ff, COLS), BF16),
                 pltpu.VMEM((2, COLS, fs), BF16),
                 pltpu.VMEM((2, fs, COLS), BF16),
-                dma((2, nc, hops)), dma((2, hops)), dma((nc,)), dma(()), dma((nc,)), dma(()), dma((2,)),
+                dma((2, nc, hops)), dma((2, hops)), dma((nc,)), dma(()), dma((nc,)), dma(()), dma((3,)),
                 dma((2, nc, hops)), dma((nc,)), dma((2,)), dma((2,)),
                 dma((2,)), dma((2,)), dma((2,)), dma((2,)),
             ],
             compiler_params=pltpu.CompilerParams(collective_id=0, has_side_effects=True, vmem_limit_bytes=VMEM_BYTES),
             cost_estimate=pl.CostEstimate(flops=flops, bytes_accessed=2 * (w_in.size + w_out.size + shared_in.size + shared_out.size), transcendentals=0),
-        )(x_loc, tab, w_in, w_out, shared_in, shared_out)
+        )(x_loc, idx_loc.T, gate_loc.T, w_in, w_out, shared_in, shared_out)
 
     tok_spec = P(('dp', 'ep'), None)
     expert_spec = P('ep', None, None)

time: 134 us -> 118 us (0.88)
  Pallas kernels: 129 us -> 115 us
  other arithmetic: 2.14 us -> 0 us
    pallas_call x1, Pallas kernels: 129 us -> 115 us  [local_layer(): pl.pallas_call(functools.partial(moe_kernel, chips, cap, top_k), out_shap...]
    select_n x1 -> x0, other arithmetic: 1.44 us -> none  [local_layer(): tab = jnp.where(side, jnp.concatenate([tab, tab], axis=1), 0.0)]
where the time goes in v3:
time: 118 us; the launch traced here: 117 us
  Pallas kernels  115 us (97%)
  local copies, waits for them, and re-layouts  1.72 us (1%)
    pallas_call x1, Pallas kernels, local_layer(): pl.pallas_call(functools.partial(moe_kernel, chips, cap, top_k), out_shap...  115 us

profile of v3, /device:TPU:21, one launch (start us, length us, event | category | flops | bytes accessed | tf_op | source)
XLA Modules:
  0.0 117.2 jit_solution(10140407305134674253)
XLA Ops:
  0.0 115.4 %shard_map.73 = bf16[64,2560]{1,0:T(8,128)(2,1)} custom-call(bf16[64,2560]{1,0:T(8,128)(2,1)} %x_hbm.1, s32[6,64]{1,0:T(8,128)} %bitcast.2, f32[6,64]{1,0:T(8,128)} %bitcast.3, bf16[4,2560,1536]{2,1,0:T(8,128)(2,1)} %wi_hbm.1, bf16[4,1536,2560]{2,1,0:T(8,128)(2,1)} %wo_hbm.1, bf16[2560,3072]{1,0:T(8,128)(2,1)} %si_hbm.1, bf16[3072,2560]{1,0:T(8,128)(2,1)} %so_hbm.1), custom_call_target="tpu_custom_call" | custom-call | flops 18119393280 | bytes 94371840 | tf_op jit(solution)/shard_map/pallas_call | solution.py:387
  115.4 1.7 %copy.9 = bf16[64,2560]{1,0:T(8,128)(2,1)} copy(bf16[64,2560]{1,0:T(8,128)(2,1)} %shard_map.73) | data formatting | bytes 655360

commit v4 on v3

--- a/solution.py
+++ b/solution.py
@@ -11,8 +11,10 @@
 COLS = 256
 LEAD = 4
 AG_LAG = 2
-RS_LAG = 2
+RS_LAGS = (1, 3, 5, 9, 11)
 PAIR = 2
+SI_SLOTS = 4
+SI_EARLY = 4
 CORES = 2
 ABSENT = -4096.0
 VMEM_BYTES = 67_000_000
@@ -26,7 +28,7 @@
 
 def moe_kernel(chips, cap, top_k,
                x_hbm, idx_hbm, top_hbm, wi_hbm, wo_hbm, si_hbm, so_hbm, y_ref,
-               x_all, idx_v, top_v, tabs, picks, codes, pick_mat, gate_mat, xg, hacc, h, outs, pbuf, ppush, prec, rbuf,
+               x_all, idx_v, top_v, tabs, picks, codes, pick_mat, gate_mat, xg, hacc, h, outs, pbuf, part, ppush, rbuf,
                sacc, s_act, u_all, wi_buf, wo_buf, si_buf, so_buf,
                ag_recv, tab_recv, ag_part, tab_part, ag_send, tab_send, own_sem,
                rs_recv, rs_send, pp_send, pp_recv, wi_sem, wo_sem, si_sem, so_sem):
@@ -94,7 +96,7 @@
         return pltpu.make_async_copy(wo_hbm.at[:, :, pl.ds(pl.multiple_of(w * COLS, COLS), COLS)], wo_buf.at[w % 2], wo_sem.at[w % 2])
 
     def si_copy(w):
-        return pltpu.make_async_copy(si_hbm.at[pl.ds(pl.multiple_of(w * COLS, COLS), COLS), :], si_buf.at[w % 2], si_sem.at[w % 2])
+        return pltpu.make_async_copy(si_hbm.at[pl.ds(pl.multiple_of(w * COLS, COLS), COLS), :], si_buf.at[w % SI_SLOTS], si_sem.at[w % SI_SLOTS])
 
     def so_copy(w):
         return pltpu.make_async_copy(so_hbm.at[:, pl.ds(pl.multiple_of(w * COLS, COLS), COLS)], so_buf.at[w % 2], so_sem.at[w % 2])
@@ -103,10 +105,8 @@
         pltpu.make_async_copy(x_hbm.at[:, pl.ds(w * COLS, COLS)], xrows(w, z), own_sem.at[0]).start()
     pltpu.make_async_copy(idx_hbm, idx_v, own_sem.at[1]).start()
     pltpu.make_async_copy(top_hbm, top_v, own_sem.at[2]).start()
-    for w in range(2):
+    for w in range(min(SI_SLOTS, nc)):
         si_copy(w).start()
-    for w in range(2):
-        wi_copy(w).start()
 
     barrier = pltpu.get_barrier_semaphore()
     for dev in (nxt, prv, partner):
@@ -132,10 +132,24 @@
             tab_copy(1, False, False).start()
             tab_push(z).start()
         ag_push(w, z).start()
-    for w in range(2):
-        wo_copy(w).start()
-        so_copy(w).start()
-
+
+    def shared_in(v):
+        si_copy(v).wait()
+        own = x_all[v, pl.ds(pl.multiple_of((c * chips + z) * rows, rows), rows), :]
+        sacc[...] += jnp.dot(own, si_buf[v % SI_SLOTS], preferred_element_type=F32)
+
+        @pl.when(v + SI_SLOTS < nc)
+        def _():
+            si_copy(v + SI_SLOTS).start()
+
+    sacc[...] = jnp.zeros_like(sacc)
+
+    def early_step(v, carry):
+        shared_in(v)
+        return carry
+
+    lax.fori_loop(0, SI_EARLY, early_step, 0)
+    wi_copy(0).start()
     hacc[...] = jnp.zeros_like(hacc)
 
     def build_tables():
@@ -184,8 +198,19 @@
 
     ag_span = (hops - 1) * AG_LAG
 
+    def expert_in(m, lo):
+        @pl.when(m < nc // PAIR - 1)
+        def _():
+            for e in range(lo, lo + experts // 2):
+                hacc[e] += jnp.dot(xg[e], wi_buf[m % 2, e], preferred_element_type=F32)
+
+        @pl.when(m == nc // PAIR - 1)
+        def _():
+            for e in range(lo, lo + experts // 2):
+                h[e] = gelu(hacc[e] + jnp.dot(xg[e], wi_buf[m % 2, e], preferred_element_type=F32)).astype(BF16)
+
     def in_step(j, carry):
-        for k in range(hops - 1, 0, -1):
+        for k in range(1, hops):
             w = j - (k - 1) * AG_LAG
 
             @pl.when((w >= 0) & (w < nc))
@@ -212,26 +237,19 @@
             ag_copy(w, 1, False).start()
             ag_push(w, z).start()
 
-        for q in range(2):
-            v = 2 * j + q
-
-            @pl.when(v < nc)
-            def _():
-                si_copy(v).wait()
-                mine = x_all[v, pl.ds(pl.multiple_of((c * chips + z) * rows, rows), rows), :]
-                part = jnp.dot(mine, si_buf[v % 2], preferred_element_type=F32)
-
-                @pl.when(v == 0)
-                def _():
-                    sacc[...] = part
-
-                @pl.when(v > 0)
-                def _():
-                    sacc[...] += part
-
-                @pl.when(v + 2 < nc)
-                def _():
-                    si_copy(v + 2).start()
+        @pl.when(j == 3)
+        def _():
+            wi_copy(1).start()
+
+        @pl.when(j == 7)
+        def _():
+            for v in range(2):
+                wo_copy(v).start()
+                so_copy(v).start()
+
+        @pl.when(j + SI_EARLY < nc)
+        def _():
+            shared_in(j + SI_EARLY)
 
         w = j - ag_span
 
@@ -261,16 +279,14 @@
                 pltpu.make_async_copy(theirs, theirs, ag_part.at[v]).wait()
                 gather(v, 1, part)
             wi_copy(m).wait()
-
-            @pl.when(w < nc - 1)
-            def _():
-                for e in range(experts):
-                    hacc[e] += jnp.dot(xg[e], wi_buf[m % 2, e], preferred_element_type=F32)
-
-            @pl.when(w == nc - 1)
-            def _():
-                for e in range(experts):
-                    h[e] = gelu(hacc[e] + jnp.dot(xg[e], wi_buf[m % 2, e], preferred_element_type=F32)).astype(BF16)
+            expert_in(m, 0)
+
+        v = w - 1
+
+        @pl.when((v >= 0) & (v < nc) & (v % PAIR == PAIR - 1))
+        def _():
+            m = v // PAIR
+            expert_in(m, experts // 2)
 
             @pl.when(m + 2 < nc // PAIR)
             def _():
@@ -278,7 +294,7 @@
 
         return carry
 
-    lax.fori_loop(0, nc + ag_span, in_step, 0)
+    lax.fori_loop(0, nc + ag_span + 1, in_step, 0)
 
     s_act[...] = gelu(sacc[...]).astype(BF16)
 
@@ -293,34 +309,11 @@
         return remote(prow(w, s, lo, cnt), rbuf.at[d, w, k - 1, pl.ds(lo, cnt)], rs_send.at[w], rs_recv.at[d, w, k - 1], nxt if up else prv)
 
     def push_copy(w):
-        return remote(ppush.at[w % 2], prec.at[w % 2], pp_send.at[w % 2], pp_recv.at[w % 2], partner)
+        return remote(ppush.at[w % 2], pbuf.at[w], pp_send.at[w % 2], pp_recv.at[w], partner)
 
     def out_step(i, carry):
-        @pl.when(i < nc)
-        def _():
-            wo_copy(i).wait()
-            for e in range(experts):
-                o = jnp.dot(h[e], wo_buf[i % 2, e], preferred_element_type=F32).astype(BF16)
-                outs[0, e * slots:(e + 1) * slots, :] = o[:slots]
-                outs[1, e * slots:(e + 1) * slots, :] = o[slots:]
-
-            @pl.when(i >= 2)
-            def _():
-                push_copy(i).wait_send()
-
-            ppush[i % 2] = jnp.dot(gate_mat[1], outs[1], preferred_element_type=F32)
-            push_copy(i).start()
-            pbuf[i] = jnp.dot(gate_mat[0], outs[0], preferred_element_type=F32)
-            so_copy(i).wait()
-            u_all[i] = jnp.dot(s_act[...], so_buf[i % 2], preferred_element_type=F32)
-
-            @pl.when(i + 2 < nc)
-            def _():
-                wo_copy(i + 2).start()
-                so_copy(i + 2).start()
-
         for k in range(hops - 1, 0, -1):
-            w = i - k * RS_LAG
+            w = i - RS_LAGS[k]
 
             @pl.when((w >= 0) & (w < nc))
             def _():
@@ -335,12 +328,37 @@
 
         @pl.when(i < nc)
         def _():
-            push_copy(i).wait_recv()
-            pbuf[i] += prec[i % 2]
-            rs_copy(i, 1, True).start()
-            rs_copy(i, 1, False).start()
-
-        w = i - hops * RS_LAG
+            wo_copy(i).wait()
+            for e in range(experts):
+                o = jnp.dot(h[e], wo_buf[i % 2, e], preferred_element_type=F32).astype(BF16)
+                outs[0, e * slots:(e + 1) * slots, :] = o[:slots]
+                outs[1, e * slots:(e + 1) * slots, :] = o[slots:]
+
+            @pl.when(i >= 2)
+            def _():
+                push_copy(i).wait_send()
+
+            ppush[i % 2] = jnp.dot(gate_mat[1], outs[1], preferred_element_type=F32)
+            push_copy(i).start()
+            part[i % 2] = jnp.dot(gate_mat[0], outs[0], preferred_element_type=F32)
+            so_copy(i).wait()
+            u_all[i] = jnp.dot(s_act[...], so_buf[i % 2], preferred_element_type=F32)
+
+            @pl.when(i + 2 < nc)
+            def _():
+                wo_copy(i + 2).start()
+                so_copy(i + 2).start()
+
+        w = i - RS_LAGS[0]
+
+        @pl.when((w >= 0) & (w < nc))
+        def _():
+            push_copy(w).wait_recv()
+            pbuf[w] += part[w % 2]
+            rs_copy(w, 1, True).start()
+            rs_copy(w, 1, False).start()
+
+        w = i - RS_LAGS[hops]
 
         @pl.when(w >= 0)
         def _():
@@ -351,7 +369,7 @@
 
         return carry
 
-    lax.fori_loop(0, nc + hops * RS_LAG, out_step, 0)
+    lax.fori_loop(0, nc + RS_LAGS[hops], out_step, 0)
 
     def drain(w, carry):
         sent = x_all.at[w, pl.ds(0, (2 * chips - 1) * rows)]
@@ -411,11 +429,11 @@
                 pltpu.VMEM((nc, rows, COLS), F32),
                 pltpu.VMEM((2, experts, PAIR * COLS, ff), BF16),
                 pltpu.VMEM((2, experts, ff, COLS), BF16),
-                pltpu.VMEM((2, COLS, fs), BF16),
+                pltpu.VMEM((SI_SLOTS, COLS, fs), BF16),
                 pltpu.VMEM((2, fs, COLS), BF16),
                 dma((2, nc, hops)), dma((2, hops)), dma((nc,)), dma(()), dma((nc,)), dma(()), dma((3,)),
-                dma((2, nc, hops)), dma((nc,)), dma((2,)), dma((2,)),
-                dma((2,)), dma((2,)), dma((2,)), dma((2,)),
+                dma((2, nc, hops)), dma((nc,)), dma((2,)), dma((nc,)),
+                dma((2,)), dma((2,)), dma((SI_SLOTS,)), dma((2,)),
             ],
             compiler_params=pltpu.CompilerParams(collective_id=0, has_side_effects=True, vmem_limit_bytes=VMEM_BYTES),
             cost_estimate=pl.CostEstimate(flops=flops, bytes_accessed=2 * (w_in.size + w_out.size + shared_in.size + shared_out.size), transcendentals=0),

time: 118 us -> 114 us (0.966)
  Pallas kernels: 115 us -> 112 us
    pallas_call x1, Pallas kernels: 115 us -> 112 us  [local_layer(): pl.pallas_call(functools.partial(moe_kernel, chips, cap, top_k), out_shap...]
where the time goes in v4:
time: 114 us; the launch traced here: 113 us
  Pallas kernels  112 us (98%)
  local copies, waits for them, and re-layouts  1.72 us (2%)
    pallas_call x1, Pallas kernels, local_layer(): pl.pallas_call(functools.partial(moe_kernel, chips, cap, top_k), out_shap...  112 us

profile of v4, /device:TPU:21, one launch (start us, length us, event | category | flops | bytes accessed | tf_op | source)
XLA Modules:
  0.0 113.4 jit_solution(10298601296383751214)
XLA Ops:
  0.0 111.6 %shard_map.73 = bf16[64,2560]{1,0:T(8,128)(2,1)} custom-call(bf16[64,2560]{1,0:T(8,128)(2,1)} %x_hbm.1, s32[6,64]{1,0:T(8,128)} %bitcast.2, f32[6,64]{1,0:T(8,128)} %bitcast.3, bf16[4,2560,1536]{2,1,0:T(8,128)(2,1)} %wi_hbm.1, bf16[4,1536,2560]{2,1,0:T(8,128)(2,1)} %wo_hbm.1, bf16[2560,3072]{1,0:T(8,128)(2,1)} %si_hbm.1, bf16[3072,2560]{1,0:T(8,128)(2,1)} %so_hbm.1), custom_call_target="tpu_custom_call" | custom-call | flops 18119393280 | bytes 94371840 | tf_op jit(solution)/shard_map/pallas_call | solution.py:405
  111.6 1.7 %copy.9 = bf16[64,2560]{1,0:T(8,128)(2,1)} copy(bf16[64,2560]{1,0:T(8,128)(2,1)} %shard_map.73) | data formatting | bytes 655360

commit v5 on v4

v5 whole, which is shorter than its diff:
```python
import functools

import jax
import jax.numpy as jnp
from jax import lax
from jax.experimental import pallas as pl
from jax.experimental.pallas import tpu as pltpu
from jax.sharding import PartitionSpec as P

LOAD_MULT = 3
COLS = 256
LEAD = 5
AG_LAGS = (0, 4, 8, 12)
AG_SHIFT = 12
RS_LAGS = (0, 2, 4, 9, 17)
PAIR = 2
IN_FIRST = 15
OUT_OFF = 0
SI_SLOTS = 4
SI_EARLY = 2
WI_AT, SO_AT, WO_AT = 3, 8, 14
CORES = 2
ABSENT = -4096.0
VMEM_BYTES = 67_000_000
F32 = jnp.float32
BF16 = jnp.bfloat16


def gelu(z):
    return 0.5 * z * (1.0 + jnp.tanh(0.7978845608028654 * (z + 0.044715 * (z * z * z))))


def moe_kernel(chips, cap, top_k,
               x_hbm, idx_hbm, top_hbm, wi_hbm, wo_hbm, si_hbm, so_hbm, y_ref,
               x_all, idx_v, top_v, tabs, picks, codes, pick_mat, gate_mat, xg, hacc, h, outs, pbuf, part, rbuf,
               sacc, s_act, u_all, wi_buf, wo_buf, si_buf, so_buf,
               ag_recv, tab_recv, ag_part, tab_part, ag_send, tab_send, own_sem,
               rs_recv, rs_send, pp_send, pp_recv, wi_sem, wo_sem, si_sem, so_sem):
    rows, d_model = x_hbm.shape
    experts = wi_hbm.shape[0]
    nc = d_model // COLS
    hops = chips // 2
    pairs_in = nc // PAIR
    half = rows // 2
    group_rows = chips * rows
    slots = chips * cap

    ep = lax.axis_index('ep')
    z, c = ep // CORES, ep % CORES
    first = lax.axis_index('dp') * (chips * CORES)
    partner = first + z * CORES + (1 - c)
    nxt = first + ((z + 1) % chips) * CORES + c
    prv = first + ((z + chips - 1) % chips) * CORES + c
    near = [(z + off) % chips for off in range(chips)]

    def chip(off):
        return near[off % chips]

    def xrows(w, s, lo=0, count=None):
        base = (c * chips + s) * rows + lo
        return x_all.at[w, pl.ds(pl.multiple_of(base, half), rows if count is None else count)]

    def tblk(s, lo=0, count=None):
        t = tabs.at[c * chips + s]
        return t if count is None else t.at[pl.ds(lo, count)]

    def remote(src, dst, ssem, rsem, dev):
        return pltpu.make_async_remote_copy(src_ref=src, dst_ref=dst, send_sem=ssem, recv_sem=rsem, device_id=dev, device_id_type=pl.DeviceIdType.LOGICAL)

    def ag_copy(w, k, up):
        s = chip(-(k - 1)) if up else chip(k - 1)
        lo, cnt = (0, None) if k < hops else ((0, half) if up else (half, half))
        ref = xrows(w, s, lo, cnt)
        return remote(ref, ref, ag_send.at[w], ag_recv.at[0 if up else 1, w, k - 1], nxt if up else prv)

    def ag_arrival(w, k, up):
        s = chip(-k) if up else chip(k)
        lo, cnt = (0, None) if k < hops else ((0, half) if up else (half, half))
        ref = xrows(w, s, lo, cnt)
        return remote(ref, ref, ag_send.at[w], ag_recv.at[0 if up else 1, w, k - 1], nxt if up else prv)

    def tab_copy(k, up, arrival):
        off = k if arrival else k - 1
        s = chip(-off) if up else chip(off)
        lo, cnt = (0, None) if k < hops else ((0, 8) if up else (8, 8))
        ref = tblk(s, lo, cnt)
        return remote(ref, ref, tab_send, tab_recv.at[0 if up else 1, k - 1], nxt if up else prv)

    def ag_push(w, s):
        ref = xrows(w, s)
        return remote(ref, ref, ag_send.at[w], ag_part.at[w], partner)

    def tab_push(s):
        ref = tblk(s)
        return remote(ref, ref, tab_send, tab_part, partner)

    def wi_copy(w):
        return pltpu.make_async_copy(wi_hbm.at[:, pl.ds(pl.multiple_of(w % pairs_in * (PAIR * COLS), COLS), PAIR * COLS), :], wi_buf.at[w % 2], wi_sem.at[w % 2])

    def wo_copy(w):
        return pltpu.make_async_copy(wo_hbm.at[:, :, pl.ds(pl.multiple_of(w % nc * COLS, COLS), COLS)], wo_buf.at[w % 2], wo_sem.at[w % 2])

    def si_copy(w):
        return pltpu.make_async_copy(si_hbm.at[pl.ds(pl.multiple_of(w * COLS, COLS), COLS), :], si_buf.at[w % SI_SLOTS], si_sem.at[w % SI_SLOTS])

    def so_copy(w):
        return pltpu.make_async_copy(so_hbm.at[:, pl.ds(pl.multiple_of(w * COLS, COLS), COLS)], so_buf.at[w % 2], so_sem.at[w % 2])

    for w in range(nc):
        pltpu.make_async_copy(x_hbm.at[:, pl.ds(w * COLS, COLS)], xrows(w, z), own_sem.at[0]).start()
    pltpu.make_async_copy(idx_hbm, idx_v, own_sem.at[1]).start()
    pltpu.make_async_copy(top_hbm, top_v, own_sem.at[2]).start()
    for w in range(min(SI_SLOTS, nc)):
        si_copy(w).start()

    barrier = pltpu.get_barrier_semaphore()
    for dev in (nxt, prv, partner):
        pl.semaphore_signal(barrier, inc=1, device_id=dev, device_id_type=pl.DeviceIdType.LOGICAL)
    pl.semaphore_wait(barrier, 3)

    pltpu.make_async_copy(idx_hbm, idx_v, own_sem.at[1]).wait()
    pltpu.make_async_copy(top_hbm, top_v, own_sem.at[2]).wait()
    right = lax.broadcasted_iota(jnp.int32, (top_k, 2 * rows), 1) >= rows
    side = right == (z % 2 == 1)
    ids, gts = idx_v[...].astype(F32), top_v[...]
    mine = tabs.at[c * chips + z]
    mine[...] = jnp.zeros_like(mine)
    mine[0:top_k, :] = jnp.where(side, jnp.concatenate([ids, ids], axis=1), 0.0)
    mine[8:8 + top_k, :] = jnp.where(side, jnp.concatenate([gts, gts], axis=1), 0.0)
    own_all = x_all.at[0, pl.ds(0, nc * rows)]
    pltpu.make_async_copy(own_all, own_all, own_sem.at[0]).wait()
    def ag_own(w):
        ag_copy(w, 1, True).start()
        ag_copy(w, 1, False).start()
        ag_push(w, z).start()

    @pl.when(c == 0)
    def _():
        for w in range(min(LEAD, nc)):
            ag_own(w)

    tab_copy(1, True, False).start()
    tab_copy(1, False, False).start()
    tab_push(z).start()

    def shared_in(v):
        si_copy(v).wait()
        own = x_all[v, pl.ds(pl.multiple_of((c * chips + z) * rows, rows), rows), :]
        sacc[...] += jnp.dot(own, si_buf[v % SI_SLOTS], preferred_element_type=F32)

        @pl.when(v + SI_SLOTS < nc)
        def _():
            si_copy(v + SI_SLOTS).start()

    sacc[...] = jnp.zeros_like(sacc)

    def early_step(v, carry):
        shared_in(v)
        return carry

    lax.fori_loop(0, SI_EARLY, early_step, 0)
    wi_copy(0).start()

    def build_tables(g):
        base = (ep * experts).astype(F32)
        lane = lax.broadcasted_iota(jnp.int32, (1, 2 * rows), 1)
        pairs = chips // 2
        for i in range(pairs):
            t = tabs[g * chips + 2 * i] + tabs[g * chips + 2 * i + 1]
            ids, gts = t[0:top_k], t[8:8 + top_k]
            for e in range(experts):
                hit = ids == (base + float(e))
                r = i * experts + e
                picks[r:r + 1, :] = jnp.sum(hit.astype(F32), axis=0, keepdims=True)
                codes[experts + e:experts + e + 1, i * 2 * rows:(i + 1) * 2 * rows] = jnp.sum(jnp.where(hit, gts, 0.0), axis=0, keepdims=True)
        a = lax.broadcasted_iota(jnp.int32, (2 * rows, 2 * rows), 0)
        b = lax.broadcasted_iota(jnp.int32, (2 * rows, 2 * rows), 1)
        before = ((a < b) & ((a >= rows) == (b >= rows))).astype(F32).astype(BF16)
        rank = jnp.dot(picks[...].astype(BF16), before, preferred_element_type=F32)
        for i in range(pairs):
            start = (2 * i * cap + jnp.where(lane >= rows, cap, 0)).astype(F32)
            for e in range(experts):
                r = i * experts + e
                code = jnp.where(picks[r:r + 1, :] > 0.5, rank[r:r + 1, :] + start, ABSENT)
                codes[e:e + 1, i * 2 * rows:(i + 1) * 2 * rows] = code
        slot = lax.broadcasted_iota(jnp.int32, (slots, group_rows), 0).astype(F32)
        col = lax.broadcasted_iota(jnp.int32, (2 * rows, experts * slots), 1).astype(F32)
        for e in range(experts):
            pick_mat[g, e * slots:(e + 1) * slots, :] = jnp.where(slot == codes[e:e + 1, :], 1.0, 0.0).astype(BF16)
        for i in range(pairs):
            ct = jnp.transpose(codes[:, i * 2 * rows:(i + 1) * 2 * rows])
            acc = jnp.zeros((2 * rows, experts * slots), F32)
            for e in range(experts):
                acc = jnp.where(col == ct[:, e:e + 1] + float(e * slots), ct[:, experts + e:experts + e + 1], acc)
            gate_mat[g, i * 2 * rows:(i + 1) * 2 * rows, :] = acc.astype(BF16)

    def gather(w, g, q):
        xs = x_all[w, pl.ds(pl.multiple_of(g * group_rows, group_rows), group_rows), :]
        got = jnp.dot(pick_mat[g], xs, preferred_element_type=F32).astype(BF16)
        for e in range(experts):
            xg[e, :, q * COLS:(q + 1) * COLS] = got[e * slots:(e + 1) * slots, :]

    ag_span = AG_LAGS[hops - 1]
    out_first = IN_FIRST + nc - PAIR + OUT_OFF

    def prow(w, s, lo=0, count=None):
        return pbuf.at[w, pl.ds(pl.multiple_of(s * rows + lo, half), rows if count is None else count)]

    def rs_copy(w, k, up):
        off = hops - k + 1
        s = chip(off) if up else chip(-off)
        lo, cnt = (0, rows) if k > 1 else ((0, half) if up else (half, half))
        d = 0 if up else 1
        return remote(prow(w, s, lo, cnt), rbuf.at[d, w, k - 1, pl.ds(lo, cnt)], rs_send.at[w], rs_recv.at[d, w, k - 1], nxt if up else prv)

    def push_copy(w):
        return remote(part.at[w % 2], pbuf.at[w], pp_send.at[w % 2], pp_recv.at[w], partner)

    shift = c * nc
    ag_shift = c * AG_SHIFT

    def rs_forward(i):
        for k in range(hops - 1, 0, -1):
            w = i - RS_LAGS[k] - shift

            @pl.when((w >= 0) & (w < nc))
            def _():
                for up in (True, False):
                    rs_copy(w, k, up).wait_recv()
                    d = 0 if up else 1
                    s = chip(hops - k) if up else chip(-(hops - k))
                    lo, cnt = (0, rows) if k > 1 else ((0, half) if up else (half, half))
                    dst = prow(w, s, lo, cnt)
                    dst[...] += rbuf[d, w, k - 1, lo:lo + cnt, :]
                    rs_copy(w, k + 1, up).start()

    def rs_final(i):
        w = i - RS_LAGS[hops] - shift

        @pl.when((w >= 0) & (w < nc))
        def _():
            rs_copy(w, hops, True).wait_recv()
            rs_copy(w, hops, False).wait_recv()
            total = prow(w, z)[...] + (rbuf[0, w, hops - 1] + rbuf[1, w, hops - 1]) + u_all[w]
            y_ref[:, pl.ds(pl.multiple_of(w * COLS, COLS), COLS)] = total.astype(BF16)

    def ag_forward(j):
        for k in range(1, hops):
            w = j - AG_LAGS[k - 1] - ag_shift

            @pl.when((w >= 0) & (w < nc))
            def _():
                for up in (True, False):
                    ag_arrival(w, k, up).wait_recv()
                    ag_copy(w, k + 1, up).start()
                ag_push(w, chip(-k)).start()
                ag_push(w, chip(k)).start()

                @pl.when(w == 0)
                def _():
                    for up in (True, False):
                        tab_copy(k, up, True).wait_recv()
                        tab_copy(k + 1, up, False).start()
                    tab_push(chip(-k)).start()
                    tab_push(chip(k)).start()

        w = j + LEAD - ag_shift

        @pl.when((w >= (1 - c) * LEAD) & (w < nc))
        def _():
            ag_own(w)

        w = j - ag_span - ag_shift

        @pl.when((w >= 0) & (w < nc))
        def _():
            for up in (True, False):
                ag_arrival(w, hops, up).wait_recv()
            ag_push(w, chip(hops)).start()

            @pl.when(w == 0)
            def _():
                for up in (True, False):
                    tab_copy(hops, up, True).wait_recv()
                tab_push(chip(hops)).start()

    def shared_part(j):
        v = j + SI_EARLY

        @pl.when(v < nc)
        def _():
            shared_in(v)

        @pl.when(v == nc)
        def _():
            s_act[...] = gelu(sacc[...]).astype(BF16)

        @pl.when(j == WI_AT)
        def _():
            wi_copy(1).start()

        @pl.when(j == SO_AT - 2)
        def _():
            for q in range(2):
                so_copy(q).start()

        @pl.when(j == WO_AT)
        def _():
            for q in range(2):
                wo_copy(q).start()

        v2 = j - SO_AT

        @pl.when((v2 >= 0) & (v2 < nc))
        def _():
            so_copy(v2).wait()
            u_all[v2] = jnp.dot(s_act[...], so_buf[v2 % 2], preferred_element_type=F32)

            @pl.when(v2 + 2 < nc)
            def _():
                so_copy(v2 + 2).start()

    def in_part(j):
        p = (j - IN_FIRST) // PAIR

        @pl.when((j >= IN_FIRST) & ((j - IN_FIRST) % PAIR == 0) & (p < 2 * pairs_in))
        def _():
            g, m = p // pairs_in, p % pairs_in

            @pl.when(m == 0)
            def _():
                @pl.when(g != c)
                def _():
                    theirs = tabs.at[pl.ds((1 - c) * chips, chips)]
                    pltpu.make_async_copy(theirs, theirs, tab_part).wait()

                build_tables(g)

            @pl.when(g != c)
            def _():
                for q in range(PAIR):
                    v = m * PAIR + q
                    theirs = x_all.at[v, pl.ds(pl.multiple_of((1 - c) * group_rows, group_rows), group_rows)]
                    pltpu.make_async_copy(theirs, theirs, ag_part.at[v]).wait()

            for q in range(PAIR):
                gather(m * PAIR + q, g, q)
            wi_copy(p).wait()

            @pl.when(m == 0)
            def _():
                for e in range(experts):
                    hacc[e] = jnp.dot(xg[e], wi_buf[p % 2, e], preferred_element_type=F32)

            @pl.when((m > 0) & (m < pairs_in - 1))
            def _():
                for e in range(experts):
                    hacc[e] += jnp.dot(xg[e], wi_buf[p % 2, e], preferred_element_type=F32)

            @pl.when((m > 0) & (m == pairs_in - 1))
            def _():
                for e in range(experts):
                    h[g, e] = gelu(hacc[e] + jnp.dot(xg[e], wi_buf[p % 2, e], preferred_element_type=F32)).astype(BF16)

            @pl.when(p + 2 < 2 * pairs_in)
            def _():
                wi_copy(p + 2).start()

    def out_part(i):
        @pl.when((i >= 0) & (i < 2 * nc))
        def _():
            g, w = i // nc, i % nc
            wo_copy(i).wait()
            for e in range(experts):
                outs[e * slots:(e + 1) * slots, :] = jnp.dot(h[g, e], wo_buf[i % 2, e], preferred_element_type=F32).astype(BF16)

            @pl.when((i - 2 >= nc - shift) & (i - 2 < 2 * nc - shift))
            def _():
                push_copy(w).wait_send()

            part[w % 2] = jnp.dot(gate_mat[g], outs[...], preferred_element_type=F32)

            @pl.when(g != c)
            def _():
                push_copy(w).start()

            @pl.when(i + 2 < 2 * nc)
            def _():
                wo_copy(i + 2).start()

    def out_send(i):
        w = i - RS_LAGS[0] - shift

        @pl.when((w >= 0) & (w < nc))
        def _():
            push_copy(w).wait_recv()
            pbuf[w] += part[w % 2]
            rs_copy(w, 1, True).start()
            rs_copy(w, 1, False).start()

    def tick(j, carry):
        i = j - out_first
        ag_forward(j)
        shared_part(j)
        in_part(j)
        rs_forward(i)
        out_part(i)
        out_send(i)
        rs_final(i)
        return carry

    lax.fori_loop(0, out_first + 2 * nc + RS_LAGS[hops], tick, 0)

    def drain(w, carry):
        sent = x_all.at[w, pl.ds(0, (2 * chips - 1) * rows)]
        pltpu.make_async_copy(sent, sent, ag_send.at[w]).wait()
        sums = pbuf.at[w, pl.ds(0, (chips - 1) * rows)]
        pltpu.make_async_copy(sums, sums, rs_send.at[w]).wait()
        return carry

    lax.fori_loop(0, nc, drain, 0)
    sent = tabs.at[pl.ds(0, 2 * chips - 1)]
    pltpu.make_async_copy(sent, sent, tab_send).wait()

    @pl.when(c == 0)
    def _():
        for w in range(2):
            push_copy(w).wait_send()


def solution(mesh):
    group_size = mesh.shape['ep']
    chips = group_size // CORES
    hops = chips // 2

    def local_layer(x_loc, idx_loc, gate_loc, w_in, w_out, shared_in, shared_out):
        rows, top_k = idx_loc.shape
        d_model = x_loc.shape[1]
        experts, _, ff = w_in.shape
        fs = shared_in.shape[1]
        num_experts = experts * group_size
        cap = min(rows, LOAD_MULT * rows * top_k // num_experts)
        slots = chips * cap
        nc = d_model // COLS
        any_spec = pl.BlockSpec(memory_space=pl.ANY)
        dma = pltpu.SemaphoreType.DMA
        flops = 2 * group_size * cap * experts * d_model * ff * 2
        return pl.pallas_call(
            functools.partial(moe_kernel, chips, cap, top_k),
            out_shape=jax.ShapeDtypeStruct((rows, d_model), BF16),
            in_specs=[any_spec] * 7,
            out_specs=pl.BlockSpec(memory_space=pltpu.VMEM),
            scratch_shapes=[
                pltpu.VMEM((nc, group_size * rows, COLS), BF16),
                pltpu.VMEM((top_k, rows), jnp.int32),
                pltpu.VMEM((top_k, rows), F32),
                pltpu.VMEM((group_size, 16, 2 * rows), F32),
                pltpu.VMEM((hops * experts, 2 * rows), F32),
                pltpu.VMEM((2 * experts, chips * rows), F32),
                pltpu.VMEM((2, experts * slots, chips * rows), BF16),
                pltpu.VMEM((2, chips * rows, experts * slots), BF16),
                pltpu.VMEM((experts, slots, PAIR * COLS), BF16),
                pltpu.VMEM((experts, slots, ff), F32),
                pltpu.VMEM((2, experts, slots, ff), BF16),
                pltpu.VMEM((experts * slots, COLS), BF16),
                pltpu.VMEM((nc, chips * rows, COLS), F32),
                pltpu.VMEM((2, chips * rows, COLS), F32),
                pltpu.VMEM((2, nc, hops, rows, COLS), F32),
                pltpu.VMEM((rows, fs), F32),
                pltpu.VMEM((rows, fs), BF16),
                pltpu.VMEM((nc, rows, COLS), F32),
                pltpu.VMEM((2, experts, PAIR * COLS, ff), BF16),
                pltpu.VMEM((2, experts, ff, COLS), BF16),
                pltpu.VMEM((SI_SLOTS, COLS, fs), BF16),
                pltpu.VMEM((2, fs, COLS), BF16),
                dma((2, nc, hops)), dma((2, hops)), dma((nc,)), dma(()), dma((nc,)), dma(()), dma((3,)),
                dma((2, nc, hops)), dma((nc,)), dma((2,)), dma((nc,)),
                dma((2,)), dma((2,)), dma((SI_SLOTS,)), dma((2,)),
            ],
            compiler_params=pltpu.CompilerParams(collective_id=0, has_side_effects=True, vmem_limit_bytes=VMEM_BYTES),
            cost_estimate=pl.CostEstimate(flops=flops, bytes_accessed=2 * (w_in.size + w_out.size + shared_in.size + shared_out.size), transcendentals=0),
        )(x_loc, idx_loc.T, gate_loc.T, w_in, w_out, shared_in, shared_out)

    tok_spec = P(('dp', 'ep'), None)
    expert_spec = P('ep', None, None)
    whole_spec = P(None, None)
    return jax.shard_map(local_layer, mesh=mesh, in_specs=(tok_spec, tok_spec, tok_spec, expert_spec, expert_spec, whole_spec, whole_spec), out_specs=tok_spec, check_vma=False)
```

time: 114 us -> 112 us (0.982)
  Pallas kernels: 112 us -> 110 us
    pallas_call x1, Pallas kernels: 112 us -> 110 us  [local_layer(): pl.pallas_call(functools.partial(moe_kernel, chips, cap, top_k), out_shap...]
where the time goes in v5:
time: 112 us
  Pallas kernels  110 us (98%)
  local copies, waits for them, and re-layouts  1.72 us (2%)
    pallas_call x1, Pallas kernels, local_layer(): pl.pallas_call(functools.partial(moe_kernel, chips, cap, top_k), out_shap...  110 us

profile of v5, /device:TPU:21, one launch (start us, length us, event | category | flops | bytes accessed | tf_op | source)
XLA Modules:
  0.0 112.1 jit_solution(15374876674053936007)
XLA Ops:
  0.0 110.3 %shard_map.73 = bf16[64,2560]{1,0:T(8,128)(2,1)} custom-call(bf16[64,2560]{1,0:T(8,128)(2,1)} %x_hbm.1, s32[6,64]{1,0:T(8,128)} %bitcast.2, f32[6,64]{1,0:T(8,128)} %bitcast.3, bf16[4,2560,1536]{2,1,0:T(8,128)(2,1)} %wi_hbm.1, bf16[4,1536,2560]{2,1,0:T(8,128)(2,1)} %wo_hbm.1, bf16[2560,3072]{1,0:T(8,128)(2,1)} %si_hbm.1, bf16[3072,2560]{1,0:T(8,128)(2,1)} %so_hbm.1), custom_call_target="tpu_custom_call" | custom-call | flops 18119393280 | bytes 94371840 | tf_op jit(solution)/shard_map/pallas_call | solution.py:448
  110.3 1.7 %copy.9 = bf16[64,2560]{1,0:T(8,128)(2,1)} copy(bf16[64,2560]{1,0:T(8,128)(2,1)} %shard_map.73) | data formatting | bytes 655360

commit v6 on v5

--- a/solution.py
+++ b/solution.py
@@ -9,19 +9,20 @@
 
 LOAD_MULT = 3
 COLS = 256
-LEAD = 5
-AG_LAGS = (0, 4, 8, 12)
+LEAD = 8
+AG_LAGS = (0, 5, 10, 14)
 AG_SHIFT = 12
-RS_LAGS = (0, 2, 4, 9, 17)
+RS_LAGS = (0, 3, 5, 9, 13)
 PAIR = 2
-IN_FIRST = 15
+IN_FIRST = 17
 OUT_OFF = 0
 SI_SLOTS = 4
-SI_EARLY = 2
-WI_AT, SO_AT, WO_AT = 3, 8, 14
+WO_SLOTS = 3
+SI_EARLY = 4
+WI_AT, SO_AT, WO_AT = 3, 6, 14
 CORES = 2
 ABSENT = -4096.0
-VMEM_BYTES = 67_000_000
+VMEM_BYTES = 65_000_000
 F32 = jnp.float32
 BF16 = jnp.bfloat16
 
@@ -98,7 +99,7 @@
         return pltpu.make_async_copy(wi_hbm.at[:, pl.ds(pl.multiple_of(w % pairs_in * (PAIR * COLS), COLS), PAIR * COLS), :], wi_buf.at[w % 2], wi_sem.at[w % 2])
 
     def wo_copy(w):
-        return pltpu.make_async_copy(wo_hbm.at[:, :, pl.ds(pl.multiple_of(w % nc * COLS, COLS), COLS)], wo_buf.at[w % 2], wo_sem.at[w % 2])
+        return pltpu.make_async_copy(wo_hbm.at[:, :, pl.ds(pl.multiple_of(w % nc * COLS, COLS), COLS)], wo_buf.at[w % WO_SLOTS], wo_sem.at[w % WO_SLOTS])
 
     def si_copy(w):
         return pltpu.make_async_copy(si_hbm.at[pl.ds(pl.multiple_of(w * COLS, COLS), COLS), :], si_buf.at[w % SI_SLOTS], si_sem.at[w % SI_SLOTS])
@@ -220,7 +221,7 @@
     ag_shift = c * AG_SHIFT
 
     def rs_forward(i):
-        for k in range(hops - 1, 0, -1):
+        for k in range(1, hops):
             w = i - RS_LAGS[k] - shift
 
             @pl.when((w >= 0) & (w < nc))
@@ -245,7 +246,7 @@
             y_ref[:, pl.ds(pl.multiple_of(w * COLS, COLS), COLS)] = total.astype(BF16)
 
     def ag_forward(j):
-        for k in range(1, hops):
+        for k in range(hops - 1, 0, -1):
             w = j - AG_LAGS[k - 1] - ag_shift
 
             @pl.when((w >= 0) & (w < nc))
@@ -306,7 +307,7 @@
 
         @pl.when(j == WO_AT)
         def _():
-            for q in range(2):
+            for q in range(WO_SLOTS):
                 wo_copy(q).start()
 
         v2 = j - SO_AT
@@ -372,7 +373,7 @@
             g, w = i // nc, i % nc
             wo_copy(i).wait()
             for e in range(experts):
-                outs[e * slots:(e + 1) * slots, :] = jnp.dot(h[g, e], wo_buf[i % 2, e], preferred_element_type=F32).astype(BF16)
+                outs[e * slots:(e + 1) * slots, :] = jnp.dot(h[g, e], wo_buf[i % WO_SLOTS, e], preferred_element_type=F32).astype(BF16)
 
             @pl.when((i - 2 >= nc - shift) & (i - 2 < 2 * nc - shift))
             def _():
@@ -384,9 +385,9 @@
             def _():
                 push_copy(w).start()
 
-            @pl.when(i + 2 < 2 * nc)
-            def _():
-                wo_copy(i + 2).start()
+            @pl.when(i + WO_SLOTS < 2 * nc)
+            def _():
+                wo_copy(i + WO_SLOTS).start()
 
     def out_send(i):
         w = i - RS_LAGS[0] - shift
@@ -402,8 +403,8 @@
         i = j - out_first
         ag_forward(j)
         shared_part(j)
+        rs_forward(i)
         in_part(j)
-        rs_forward(i)
         out_part(i)
         out_send(i)
         rs_final(i)
@@ -447,7 +448,7 @@
         flops = 2 * group_size * cap * experts * d_model * ff * 2
         return pl.pallas_call(
             functools.partial(moe_kernel, chips, cap, top_k),
-            out_shape=jax.ShapeDtypeStruct((rows, d_model), BF16),
+            out_shape=pltpu.VMEM((rows, d_model), BF16),
             in_specs=[any_spec] * 7,
             out_specs=pl.BlockSpec(memory_space=pltpu.VMEM),
             scratch_shapes=[
@@ -470,12 +471,12 @@
                 pltpu.VMEM((rows, fs), BF16),
                 pltpu.VMEM((nc, rows, COLS), F32),
                 pltpu.VMEM((2, experts, PAIR * COLS, ff), BF16),
-                pltpu.VMEM((2, experts, ff, COLS), BF16),
+                pltpu.VMEM((WO_SLOTS, experts, ff, COLS), BF16),
                 pltpu.VMEM((SI_SLOTS, COLS, fs), BF16),
                 pltpu.VMEM((2, fs, COLS), BF16),
                 dma((2, nc, hops)), dma((2, hops)), dma((nc,)), dma(()), dma((nc,)), dma(()), dma((3,)),
                 dma((2, nc, hops)), dma((nc,)), dma((2,)), dma((nc,)),
-                dma((2,)), dma((2,)), dma((SI_SLOTS,)), dma((2,)),
+                dma((2,)), dma((WO_SLOTS,)), dma((SI_SLOTS,)), dma((2,)),
             ],
             compiler_params=pltpu.CompilerParams(collective_id=0, has_side_effects=True, vmem_limit_bytes=VMEM_BYTES),
             cost_estimate=pl.CostEstimate(flops=flops, bytes_accessed=2 * (w_in.size + w_out.size + shared_in.size + shared_out.size), transcendentals=0),

time: 112 us -> 109 us (0.973)
  Pallas kernels: 110 us -> 108 us
    pallas_call x1, Pallas kernels: 110 us -> 108 us  [local_layer(): pl.pallas_call(functools.partial(moe_kernel, chips, cap, top_k), out_shap...]
where the time goes in v6:
time: 109 us
  Pallas kernels  108 us (99%)
    pallas_call x1, Pallas kernels, local_layer(): pl.pallas_call(functools.partial(moe_kernel, chips, cap, top_k), out_shap...  108 us

profile of v6, /device:TPU:21, one launch (start us, length us, event | category | flops | bytes accessed | tf_op | source)
XLA Modules:
  0.0 109.0 jit_solution(15967447050416359742)
XLA Ops:
  0.0 108.3 %shard_map.73 = bf16[64,2560]{1,0:T(8,128)(2,1)S(1)} custom-call(bf16[64,2560]{1,0:T(8,128)(2,1)} %x_hbm.1, s32[6,64]{1,0:T(8,128)} %bitcast.2, f32[6,64]{1,0:T(8,128)} %bitcast.3, bf16[4,2560,1536]{2,1,0:T(8,128)(2,1)} %wi_hbm.1, bf16[4,1536,2560]{2,1,0:T(8,128)(2,1)} %wo_hbm.1, bf16[2560,3072]{1,0:T(8,128)(2,1)} %si_hbm.1, bf16[3072,2560]{1,0:T(8,128)(2,1)} %so_hbm.1), custom_call_target="tpu_custom_call" | custom-call | flops 18119393280 | bytes 94371840 | tf_op jit(solution)/shard_map/pallas_call | solution.py:449
  108.3 0.7 copy.9

commit v7 on v6

--- a/solution.py
+++ b/solution.py
@@ -9,12 +9,12 @@
 
 LOAD_MULT = 3
 COLS = 256
-LEAD = 8
-AG_LAGS = (0, 5, 10, 14)
-AG_SHIFT = 12
+LEAD = 6
+AG_LAGS = (0, 4, 8, 11)
+AG_SHIFT = 13
 RS_LAGS = (0, 3, 5, 9, 13)
 PAIR = 2
-IN_FIRST = 17
+IN_FIRST = 15
 OUT_OFF = 0
 SI_SLOTS = 4
 WO_SLOTS = 3
@@ -321,21 +321,26 @@
             def _():
                 so_copy(v2 + 2).start()
 
+    def table_part(j):
+        span = pairs_in * PAIR
+
+        @pl.when((j == IN_FIRST - 1) | (j == IN_FIRST + span))
+        def _():
+            g = (j - (IN_FIRST - 1)) // span
+
+            @pl.when(g != c)
+            def _():
+                theirs = tabs.at[pl.ds((1 - c) * chips, chips)]
+                pltpu.make_async_copy(theirs, theirs, tab_part).wait()
+
+            build_tables(g)
+
     def in_part(j):
         p = (j - IN_FIRST) // PAIR
 
         @pl.when((j >= IN_FIRST) & ((j - IN_FIRST) % PAIR == 0) & (p < 2 * pairs_in))
         def _():
             g, m = p // pairs_in, p % pairs_in
-
-            @pl.when(m == 0)
-            def _():
-                @pl.when(g != c)
-                def _():
-                    theirs = tabs.at[pl.ds((1 - c) * chips, chips)]
-                    pltpu.make_async_copy(theirs, theirs, tab_part).wait()
-
-                build_tables(g)
 
             @pl.when(g != c)
             def _():
@@ -404,6 +409,7 @@
         ag_forward(j)
         shared_part(j)
         rs_forward(i)
+        table_part(j)
         in_part(j)
         out_part(i)
         out_send(i)

time: 109 us -> 109 us (level)
  no operation moved by 1% of the time
where the time goes in v7:
time: 109 us
  Pallas kernels  108 us (99%)
    pallas_call x1, Pallas kernels, local_layer(): pl.pallas_call(functools.partial(moe_kernel, chips, cap, top_k), out_shap...  108 us

profile of v7, /device:TPU:21, one launch (start us, length us, event | category | flops | bytes accessed | tf_op | source)
XLA Modules:
  0.0 108.5 jit_solution(17033119361134049097)
XLA Ops:
  0.0 107.8 %shard_map.73 = bf16[64,2560]{1,0:T(8,128)(2,1)S(1)} custom-call(bf16[64,2560]{1,0:T(8,128)(2,1)} %x_hbm.1, s32[6,64]{1,0:T(8,128)} %bitcast.2, f32[6,64]{1,0:T(8,128)} %bitcast.3, bf16[4,2560,1536]{2,1,0:T(8,128)(2,1)} %wi_hbm.1, bf16[4,1536,2560]{2,1,0:T(8,128)(2,1)} %wo_hbm.1, bf16[2560,3072]{1,0:T(8,128)(2,1)} %si_hbm.1, bf16[3072,2560]{1,0:T(8,128)(2,1)} %so_hbm.1), custom_call_target="tpu_custom_call" | custom-call | flops 18119393280 | bytes 94371840 | tf_op jit(solution)/shard_map/pallas_call | solution.py:455
  107.8 0.7 copy.9
